TPU v7x, 32 devices: a whole 2x2x4 slice. The times are simulated.
32 devices in a mesh: rep: 1, dp: 32 (over x, y, z, core).
Axes of the slice: x: 2, y: 2, z: 4, core: 2. Of those that a mesh axis runs over, the one named last changes fastest.
Arguments:
- x: bfloat16 [32, 2048, 1024], P(('rep', 'dp'))
- dy: bfloat16 [32, 2048, 1024], P(('rep', 'dp'))
- w_gate: bfloat16 [2, 1024, 4096], P(None, 'dp')
- w_up: bfloat16 [2, 1024, 4096], P(None, 'dp')
- w_down: bfloat16 [2, 4096, 1024], P(None, 'dp')
- m_w_gate: float32 [2, 1024, 4096], P(None, 'dp')
- m_w_up: float32 [2, 1024, 4096], P(None, 'dp')
- m_w_down: float32 [2, 4096, 1024], P(None, 'dp')
- v_w_gate: float32 [2, 1024, 4096], P(None, 'dp')
- v_w_up: float32 [2, 1024, 4096], P(None, 'dp')
- v_w_down: float32 [2, 4096, 1024], P(None, 'dp')
Outputs:
- output 1: bfloat16 [2, 1024, 4096], P('rep', 'dp')
- output 2: bfloat16 [2, 1024, 4096], P('rep', 'dp')
- output 3: bfloat16 [2, 4096, 1024], P('rep', 'dp')
- output 4: float32 [2, 1024, 4096], P('rep', 'dp')
- output 5: float32 [2, 1024, 4096], P('rep', 'dp')
- output 6: float32 [2, 4096, 1024], P('rep', 'dp')
- output 7: float32 [2, 1024, 4096], P('rep', 'dp')
- output 8: float32 [2, 1024, 4096], P('rep', 'dp')
- output 9: float32 [2, 4096, 1024], P('rep', 'dp')
All inputs are finite; a program needn't handle non-finite values.
Results may differ from a plain program's by a relative error of at most 0.0278.
Values are sent between devices in bfloat16 or wider.
A program may use at most 2 GiB of HBM per device.

v0:
```python
import jax
import jax.numpy as jnp
from jax import lax
from jax.sharding import PartitionSpec as P

NAMES = ("w_gate", "w_up", "w_down")


def matmul(a, w):
    return jnp.dot(a, w, preferred_element_type=jnp.float32).astype(jnp.bfloat16)


def normed(h):
    wide = h.astype(jnp.float32)
    scale = lax.rsqrt(jnp.mean(wide**2, -1, keepdims=True) + 1e-6)
    return (wide * scale).astype(jnp.bfloat16)


def layer(h, w):
    a = normed(h)
    gate = jnp.dot(a, w["w_gate"], preferred_element_type=jnp.float32)
    up = jnp.dot(a, w["w_up"], preferred_element_type=jnp.float32)
    return h + matmul((jax.nn.silu(gate) * up).astype(jnp.bfloat16), w["w_down"])


def adamw(w, m, v, g):
    m = 0.9 * m + 0.1 * g
    v = 0.95 * v + 0.05 * g * g
    step = m * lax.rsqrt(v + 1e-8) + 0.1 * w
    return (w - 0.02 * step).astype(jnp.bfloat16), m, v


def clipped(gradients, sum_of_squares, count):
    factor = jnp.minimum(1.0, 0.5 * lax.rsqrt(sum_of_squares / count + 1e-30))
    return [g * factor for g in gradients]


def solution(mesh):
    def fetched(weights, number):
        return {name: lax.all_gather(w[number], "dp", axis=0, tiled=True) for name, w in zip(NAMES, weights, strict=True)}

    def step(x, dy, *arrays):
        weights, m, v = (arrays[i : i + 3] for i in (0, 3, 6))
        layers = weights[0].shape[0]
        h, kept = x[0], []
        for number in range(layers):
            kept.append(h)
            h = layer(h, fetched(weights, number))
        by_h, mine = dy[0], [None] * layers
        for number in reversed(range(layers)):
            _, back = jax.vjp(lambda w, h: layer(h, w), fetched(weights, number), kept[number])
            by_w, by_h = back(by_h)
            mine[number] = [lax.psum_scatter(by_w[name], "dp", scatter_dimension=0, tiled=True) for name in NAMES]
        gradients = [jnp.stack([mine[number][i] for number in range(layers)]).astype(jnp.float32) for i in range(3)]
        squares = lax.psum(sum(jnp.sum(g * g) for g in gradients), "dp")
        gradients = clipped(gradients, squares, lax.psum(1, "dp") * sum(g.size for g in gradients))
        new = [adamw(w.astype(jnp.float32), m, v, g) for w, m, v, g in zip(weights, m, v, gradients, strict=True)]
        return tuple(one[which] for which in range(3) for one in new)

    states, cut = P(("rep", "dp"), None, None), P(None, "dp", None)
    return jax.shard_map(
        step,
        mesh=mesh,
        in_specs=(states, states) + (cut,) * 9,
        out_specs=(P("rep", "dp", None),) * 9,
        check_vma=False,
    )
```

profile of v0, /device:TPU:0, one launch (start us, length us, event | category | flops | bytes accessed | tf_op | source)
XLA Modules:
  0.0 1579.3 jit_solution(7412972798022678024)
XLA Ops:
  7.2 1.9 fusion.94
  9.1 0.0 all-gather.15.cloned.1.call-start
  9.1 1.9 fusion.93
  11.0 0.0 all-gather.17.cloned.1.call-start
  11.1 1.9 fusion.92
  13.0 0.5 all-gather.23.cloned.1.call-update
  13.6 0.5 all-gather.21.cloned.1.call-update
  14.2 0.5 all-gather.19.cloned.1.call-update
  14.7 6.5 copy.20
  21.3 3.1 fusion.15
  24.4 6.5 copy.21
  30.9 60.5 %all-gather.13.cloned.1.call-done = bf16[1,1024,4096]{2,1,0:T(8,128)(2,1)} async-done(((bf16[1,32,4096]{2,1,0:T(8,128)(2,1)}), bf16[1,1024,4096]{2,1,0:T(8,128)(2,1)}) %all-gather.13.cloned.1.call-update) | async-done | bytes 8388624 | tf_op jit(solution)/shard_map/all_gather | solution.py:40
  91.3 24.3 %fusion.35 = f32[2048,4096]{1,0:T(8,128)} fusion(bf16[1,1024,4096]{2,1,0:T(8,128)(2,1)} %all-gather.13.cloned.1.call-done, bf16[1,2048,1024]{1,2,0:T(8,128)(2,1)} %copy.20, f32[2048]{0:T(1024)S(1)} %add_rsqrt_fusion), kind=kOutput, calls=%fused_computation.53 | convolution fusion | flops 17186160640 | bytes 46145536 | tf_op jit(solution)/shard_map/dot_general | solution.py:21
  115.7 55.2 %all-gather.15.cloned.1.call-done = bf16[1,1024,4096]{2,1,0:T(8,128)(2,1)} async-done(((bf16[1,32,4096]{2,1,0:T(8,128)(2,1)}), bf16[1,1024,4096]{2,1,0:T(8,128)(2,1)}) %all-gather.15.cloned.1.call-update) | async-done | bytes 8388624 | tf_op jit(solution)/shard_map/all_gather | solution.py:40
  170.9 39.2 %multiply_convert_fusion.1 = (bf16[2048,4096]{1,0:T(8,128)(2,1)}, f32[2048,4096]{1,0:T(8,128)}) fusion(f32[2048,4096]{1,0:T(8,128)} %fusion.35, bf16[1,1024,4096]{2,1,0:T(8,128)(2,1)} %all-gather.15.cloned.1.call-done, bf16[1,2048,1024]{1,2,0:T(8,128)(2,1)} %copy.20, f32[2048]{0:T(1024)S(1)} %add_rsqrt_fusion), kind=kOutput, calls=%fused_computation.17 | convolution fusion | flops 17236492288 | bytes 96477184 | tf_op jit(solution)/shard_map/dot_general | solution.py:22
  210.1 40.3 %all-gather.17.cloned.1.call-done = bf16[1,4096,1024]{2,1,0:T(8,128)(2,1)} async-done(((bf16[1,128,1024]{2,1,0:T(8,128)(2,1)}), bf16[1,4096,1024]{2,1,0:T(8,128)(2,1)}) %all-gather.17.cloned.1.call-update) | async-done | bytes 8388624 | tf_op jit(solution)/shard_map/all_gather | solution.py:40
  250.5 24.5 %fusion.19 = (f32[2048]{0:T(1024)S(1)}, bf16[2048,1024]{0,1:T(8,128)(2,1)}) fusion(bf16[2048,4096]{1,0:T(8,128)(2,1)} %get-tuple-element.24, bf16[1,4096,1024]{2,1,0:T(8,128)(2,1)} %all-gather.17.cloned.1.call-done, bf16[1,2048,1024]{1,2,0:T(8,128)(2,1)} %copy.20), kind=kOutput, calls=%fused_computation.37 | convolution fusion | flops 17190352896 | bytes 33562624 | tf_op jit(solution)/shard_map/dot_general | solution.py:10
  275.0 0.6 copy-done.9
  275.6 54.3 %all-gather.23.cloned.1.call-done = bf16[1,1024,4096]{2,1,0:T(8,128)(2,1)} async-done(((bf16[1,32,4096]{2,1,0:T(8,128)(2,1)}), bf16[1,1024,4096]{2,1,0:T(8,128)(2,1)}) %all-gather.23.cloned.1.call-update) | async-done | bytes 8388624 | tf_op jit(solution)/shard_map/all_gather | solution.py:40
  329.9 24.4 %fusion.22 = f32[2048,4096]{1,0:T(8,128)} fusion(bf16[1,1024,4096]{2,1,0:T(8,128)(2,1)} %all-gather.23.cloned.1.call-done, bf16[2048,1024]{0,1:T(8,128)(2,1)} %get-tuple-element.27, f32[2048]{0:T(1024)S(1)} %fusion.80), kind=kOutput, calls=%fused_computation.40 | convolution fusion | flops 17186160640 | bytes 46145536 | tf_op jit(solution)/shard_map/jvp()/dot_general | solution.py:22
  354.3 55.1 %all-gather.21.cloned.1.call-done = bf16[1,4096,1024]{2,1,0:T(8,128)(2,1)} async-done(((bf16[1,128,1024]{2,1,0:T(8,128)(2,1)}), bf16[1,4096,1024]{2,1,0:T(8,128)(2,1)}) %all-gather.21.cloned.1.call-update) | async-done | bytes 8388624 | tf_op jit(solution)/shard_map/all_gather | solution.py:40
  409.4 24.5 %convolution_convert_fusion.1 = bf16[2048,4096]{1,0:T(8,128)(2,1)} fusion(bf16[1,4096,1024]{2,1,0:T(8,128)(2,1)} %all-gather.21.cloned.1.call-done, bf16[1,2048,1024]{2,1,0:T(8,128)(2,1)} %param.12), kind=kOutput, calls=%fused_computation.25 | convolution fusion | flops 17188257792 | bytes 29360128 | tf_op jit(solution)/shard_map/transpose(jvp())/dot_general | solution.py:10
  433.8 54.9 %all-gather.19.cloned.1.call-done = bf16[1,1024,4096]{2,1,0:T(8,128)(2,1)} async-done(((bf16[1,32,4096]{2,1,0:T(8,128)(2,1)}), bf16[1,1024,4096]{2,1,0:T(8,128)(2,1)}) %all-gather.19.cloned.1.call-update) | async-done | bytes 8388624 | tf_op jit(solution)/shard_map/all_gather | solution.py:40
  488.8 46.5 %fusion.2 = (bf16[2048,4096]{1,0:T(8,128)(2,1)}, f32[2048,4096]{1,0:T(8,128)}) fusion(f32[2048,4096]{1,0:T(8,128)} %fusion.22, bf16[2048,4096]{1,0:T(8,128)(2,1)} %convolution_convert_fusion.1, bf16[1,1024,4096]{2,1,0:T(8,128)(2,1)} %all-gather.19.cloned.1.call-done, bf16[2048,1024]{0,1:T(8,128)(2,1)} %get-tuple-element.27, f32[2048]{0:T(1024)S(1)} %fusion.80), kind=kOutput, calls=%fused_computation.8 | convolution fusion | flops 17286823936 | bytes 113254400 | tf_op jit(solution)/shard_map/jvp()/dot_general | solution.py:21
  535.3 27.3 %fusion.12 = bf16[2048,1024]{0,1:T(8,128)(2,1)} fusion(bf16[2048,4096]{1,0:T(8,128)(2,1)} %convolution_convert_fusion.1, bf16[1,1024,4096]{2,1,0:T(8,128)(2,1)} %all-gather.23.cloned.1.call-done, f32[2048,4096]{1,0:T(8,128)} %get-tuple-element.29), kind=kOutput, calls=%fused_computation.21 | convolution fusion | flops 17230200832 | bytes 62914560 | tf_op jit(solution)/shard_map/transpose(jvp())/dot_general | solution.py:22
  562.6 25.1 %fusion.21 = (f32[2048]{0:T(1024)S(1)}, bf16[2048,1024]{0,1:T(8,128)(2,1)S(1)}) fusion(bf16[2048,1024]{0,1:T(8,128)(2,1)S(1)} %copy-done.1, bf16[2048,1024]{0,1:T(8,128)(2,1)} %fusion.12, bf16[2048,4096]{1,0:T(8,128)(2,1)} %get-tuple-element.28, bf16[1,1024,4096]{2,1,0:T(8,128)(2,1)} %all-gather.19.cloned.1.call-done), kind=kOutput, calls=%fused_computation.39 | convolution fusion | flops 17190352896 | bytes 37756928 | tf_op jit(solution)/shard_map/transpose(jvp())/dot_general | solution.py:21
  587.7 3.1 fusion.44
  590.9 2.0 copy-done.2
  592.9 23.2 %convolution_convert_fusion.2 = bf16[4096,1024]{1,0:T(8,128)(2,1)} fusion(bf16[2048,4096]{1,0:T(8,128)(2,1)} %get-tuple-element.24, bf16[2048,1024]{0,1:T(8,128)(2,1)S(1)} %fusion.44), kind=kOutput, calls=%fused_computation.59 | convolution fusion | flops 17184063488 | bytes 29360128 | tf_op jit(solution)/shard_map/transpose(jvp())/dot_general | solution.py:10
  616.1 30.5 %fusion.40 = bf16[4096,1024]{1,0:T(8,128)(2,1)} fusion(f32[2048,4096]{1,0:T(8,128)} %fusion.22, bf16[1,2048,1024]{2,1,0:T(8,128)(2,1)} %param.12, f32[2048,4096]{1,0:T(8,128)} %get-tuple-element.29), kind=kOutput, calls=%fused_computation.56 | convolution fusion | flops 17234395136 | bytes 79691776 | tf_op jit(solution)/shard_map/transpose(jvp())/dot_general | solution.py:10
  646.8 24.9 %convolution_convert_fusion = bf16[2048,4096]{1,0:T(8,128)(2,1)} fusion(bf16[2048,1024]{0,1:T(8,128)(2,1)} %copy-done.2, bf16[1,4096,1024]{2,1,0:T(8,128)(2,1)} %all-gather.17.cloned.1.call-done), kind=kOutput, calls=%fused_computation.24 | convolution fusion | flops 17188257792 | bytes 29360128 | tf_op jit(solution)/shard_map/transpose(jvp())/dot_general | solution.py:10
  671.6 26.9 %fusion.42 = bf16[1024,4096]{1,0:T(8,128)(2,1)} fusion(bf16[2048,4096]{1,0:T(8,128)(2,1)} %convolution_convert_fusion, f32[2048,4096]{1,0:T(8,128)} %fusion.35, bf16[1,2048,1024]{1,2,0:T(8,128)(2,1)} %copy.20, f32[2048]{0:T(1024)S(1)} %copy-done.12), kind=kOutput, calls=%fused_computation.58 | convolution fusion | flops 17240686592 | bytes 62922752 | tf_op jit(solution)/shard_map/transpose(jvp())/dot_general | solution.py:22
  698.6 0.6 copy-done.8
  699.2 26.6 %fusion.41 = bf16[1024,4096]{1,0:T(8,128)(2,1)} fusion(bf16[2048,4096]{1,0:T(8,128)(2,1)} %convolution_convert_fusion.1, bf16[2048,1024]{0,1:T(8,128)(2,1)} %get-tuple-element.27, f32[2048]{0:T(1024)S(1)} %copy-done.8, f32[2048,4096]{1,0:T(8,128)} %get-tuple-element.29), kind=kOutput, calls=%fused_computation.57 | convolution fusion | flops 17240686592 | bytes 62922752 | tf_op jit(solution)/shard_map/transpose(jvp())/dot_general | solution.py:22
  725.9 37.1 %fusion.37 = bf16[1024,4096]{1,0:T(8,128)(2,1)} fusion(f32[2048,4096]{1,0:T(8,128)} %fusion.35, f32[2048,4096]{1,0:T(8,128)} %get-tuple-element.25, bf16[2048,4096]{1,0:T(8,128)(2,1)} %convolution_convert_fusion, bf16[1,2048,1024]{1,2,0:T(8,128)(2,1)} %copy.20, f32[2048]{0:T(1024)S(1)} %copy-done.12), kind=kOutput, calls=%fused_computation.55 | convolution fusion | flops 17282629632 | bytes 96477184 | tf_op jit(solution)/shard_map/transpose(jvp())/dot_general | solution.py:21
  763.1 0.0 reduce-scatter.9.cloned.1.call-start
  763.2 22.8 %convolution_convert_fusion.3 = bf16[1024,4096]{1,0:T(8,128)(2,1)} fusion(bf16[2048,4096]{1,0:T(8,128)(2,1)} %get-tuple-element.28, bf16[2048,1024]{0,1:T(8,128)(2,1)} %get-tuple-element.27, f32[2048]{0:T(1024)S(1)} %copy-done.8), kind=kOutput, calls=%fused_computation.60 | convolution fusion | flops 17186160640 | bytes 29368320 | tf_op jit(solution)/shard_map/transpose(jvp())/dot_general | solution.py:21
  786.1 131.3 %reduce-scatter.17.cloned.1.call-done = bf16[128,1024]{1,0:T(8,128)(2,1)} async-done(((bf16[4096,1024]{1,0:T(8,128)(2,1)}), bf16[128,1024]{1,0:T(8,128)(2,1)}) %reduce-scatter.17.cloned.1.call-update) | async-done | bytes 262160 | tf_op jit(solution)/shard_map/reduce_scatter | solution.py:53
  917.4 1.9 fusion.70
  919.3 149.3 %reduce-scatter.11.cloned.1.call-done = bf16[32,4096]{1,0:T(8,128)(2,1)} async-done(((bf16[1024,4096]{1,0:T(8,128)(2,1)}), bf16[32,4096]{1,0:T(8,128)(2,1)}) %reduce-scatter.11.cloned.1.call-update) | async-done | bytes 262160 | tf_op jit(solution)/shard_map/reduce_scatter | solution.py:53
  1068.6 151.1 %reduce-scatter.13.cloned.1.call-done = bf16[32,4096]{1,0:T(8,128)(2,1)} async-done(((bf16[1024,4096]{1,0:T(8,128)(2,1)}), bf16[32,4096]{1,0:T(8,128)(2,1)}) %reduce-scatter.13.cloned.1.call-update) | async-done | bytes 262160 | tf_op jit(solution)/shard_map/reduce_scatter | solution.py:53
  1219.6 1.9 fusion.69
  1221.6 149.3 %reduce-scatter.7.cloned.1.call-done = bf16[32,4096]{1,0:T(8,128)(2,1)} async-done(((bf16[1024,4096]{1,0:T(8,128)(2,1)}), bf16[32,4096]{1,0:T(8,128)(2,1)}) %reduce-scatter.7.cloned.1.call-update) | async-done | bytes 262160 | tf_op jit(solution)/shard_map/reduce_scatter | solution.py:53
  1370.8 151.0 %reduce-scatter.9.cloned.1.call-done = bf16[32,4096]{1,0:T(8,128)(2,1)} async-done(((bf16[1024,4096]{1,0:T(8,128)(2,1)}), bf16[32,4096]{1,0:T(8,128)(2,1)}) %reduce-scatter.9.cloned.1.call-update) | async-done | bytes 262160 | tf_op jit(solution)/shard_map/reduce_scatter | solution.py:53
  1521.8 1.9 fusion.68
  1525.7 36.9 %psum.7 = f32[]{:T(128)} all-reduce(f32[]{:T(128)S(6)} %add.99), channel_id=1, replica_groups=mesh['rep'=1,'dp'=32] {'dp'}, use_global_device_ids=true, to_apply=%region_12.13 | all-reduce | flops 1 | bytes 8 | tf_op jit(solution)/shard_map/psum | solution.py:55
  1563.3 3.5 fusion.76
  1566.9 5.1 fusion.67
  (45 shorter events, 0.6 us)
Async XLA Ops:
  7.2 84.2 %all-gather.13.cloned.1.call-start = ((), (), s32[]{:S(2)}) async-start(), calls=%async_computation.12 | async-start | bytes 8650752 | tf_op jit(solution)/shard_map/all_gather | solution.py:40
  9.1 161.8 %all-gather.15.cloned.1.call-start = ((), (), s32[]{:S(2)}) async-start(), calls=%async_computation.13 | async-start | bytes 8650752 | tf_op jit(solution)/shard_map/all_gather | solution.py:40
  11.0 239.4 %all-gather.17.cloned.1.call-start = ((), (), s32[]{:S(2)}) async-start(), calls=%async_computation.14 | async-start | bytes 8650752 | tf_op jit(solution)/shard_map/all_gather | solution.py:40
  13.0 317.0 %all-gather.23.cloned.1.call-start = ((), (), s32[]{:S(2)}) async-start(), calls=%async_computation.17 | async-start | bytes 8650752 | tf_op jit(solution)/shard_map/all_gather | solution.py:40
  13.5 395.8 %all-gather.21.cloned.1.call-start = ((), (), s32[]{:S(2)}) async-start(), calls=%async_computation.16 | async-start | bytes 8650752 | tf_op jit(solution)/shard_map/all_gather | solution.py:40
  14.1 474.6 %all-gather.19.cloned.1.call-start = ((), (), s32[]{:S(2)}) async-start(), calls=%async_computation.15 | async-start | bytes 8650752 | tf_op jit(solution)/shard_map/all_gather | solution.py:40
  14.7 771.3 %reduce-scatter.15.cloned.1.call-start = ((), (), s32[]{:S(2)}) async-start(), calls=%async_computation.10 | async-start | bytes 8650752 | tf_op jit(solution)/shard_map/reduce_scatter | solution.py:53
  24.4 146.5 %copy-start.11 = (f32[2048]{0:T(1024)}, f32[2048]{0:T(1024)S(1)}, u32[]{:S(2)}) copy-start(f32[2048]{0:T(1024)S(1)} %add_rsqrt_fusion) | copy-start | bytes 24580
  275.0 0.6 copy-start.9
  275.6 312.1 %copy-start.7 = (f32[2048]{0:T(1024)}, f32[2048]{0:T(1024)S(1)}, u32[]{:S(2)}) copy-start(f32[2048]{0:T(1024)S(1)} %fusion.80) | copy-start | bytes 24580
  535.3 27.3 %copy-start.1 = (bf16[2048,1024]{0,1:T(8,128)(2,1)S(1)}, bf16[2048,1024]{0,1:T(8,128)(2,1)}, u32[]{:S(2)}) copy-start(bf16[2048,1024]{0,1:T(8,128)(2,1)} %get-tuple-element.27) | copy-start | bytes 12582916
  562.6 25.1 %copy-start.10 = (f32[2048]{0:T(1024)S(1)}, f32[2048]{0:T(1024)}, u32[]{:S(2)}) copy-start(f32[2048]{0:T(1024)} %copy-done.9) | copy-start | bytes 24580
  562.6 25.2 %copy-start = (bf16[1,2048,1024]{1,2,0:T(8,128)(2,1)S(1)}, bf16[1,2048,1024]{1,2,0:T(8,128)(2,1)}, u32[]{:S(2)}) copy-start(bf16[1,2048,1024]{1,2,0:T(8,128)(2,1)} %copy.21) | copy-start | bytes 12582916
  590.9 2.0 copy-start.2
  616.1 301.3 %reduce-scatter.17.cloned.1.call-start = ((), (), s32[]{:S(2)}) async-start(), calls=%async_computation.11 | async-start | bytes 8650752 | tf_op jit(solution)/shard_map/reduce_scatter | solution.py:53
  646.7 24.9 %copy-start.12 = (f32[2048]{0:T(1024)S(1)}, f32[2048]{0:T(1024)}, u32[]{:S(2)}) copy-start(f32[2048]{0:T(1024)} %copy-done.11) | copy-start | bytes 24580
  646.7 421.9 %reduce-scatter.11.cloned.1.call-start = ((), (), s32[]{:S(2)}) async-start(), calls=%async_computation.8 | async-start | bytes 8650752 | tf_op jit(solution)/shard_map/reduce_scatter | solution.py:53
  698.5 0.7 copy-start.8
  698.5 521.1 %reduce-scatter.13.cloned.1.call-start = ((), (), s32[]{:S(2)}) async-start(), calls=%async_computation.9 | async-start | bytes 8650752 | tf_op jit(solution)/shard_map/reduce_scatter | solution.py:53
  725.9 644.9 %reduce-scatter.7.cloned.1.call-start = ((), (), s32[]{:S(2)}) async-start(), calls=%async_computation.6 | async-start | bytes 8650752 | tf_op jit(solution)/shard_map/reduce_scatter | solution.py:53
  763.1 758.7 %reduce-scatter.9.cloned.1.call-start = ((), (), s32[]{:S(2)}) async-start(), calls=%async_computation.7 | async-start | bytes 8650752 | tf_op jit(solution)/shard_map/reduce_scatter | solution.py:53
  786.0 777.3 %copy-start.3 = (bf16[2,128,1024]{2,1,0:T(8,128)(2,1)S(1)}, bf16[2,128,1024]{2,1,0:T(8,128)(2,1)}, u32[]{:S(2)}) copy-start(bf16[2,128,1024]{2,1,0:T(8,128)(2,1)} %param.15) | copy-start | bytes 1572868
  786.0 780.9 %copy-start.4 = (bf16[2,32,4096]{2,1,0:T(8,128)(2,1)S(1)}, bf16[2,32,4096]{2,1,0:T(8,128)(2,1)}, u32[]{:S(2)}) copy-start(bf16[2,32,4096]{2,1,0:T(8,128)(2,1)} %param.13) | copy-start | bytes 1572868
  786.0 780.9 %copy-start.5 = (bf16[2,32,4096]{2,1,0:T(8,128)(2,1)S(1)}, bf16[2,32,4096]{2,1,0:T(8,128)(2,1)}, u32[]{:S(2)}) copy-start(bf16[2,32,4096]{2,1,0:T(8,128)(2,1)} %param.14) | copy-start | bytes 1572868
  786.0 780.9 %copy-start.6 = (f32[2,32,4096]{2,1,0:T(8,128)S(1)}, f32[2,32,4096]{2,1,0:T(8,128)}, u32[]{:S(2)}) copy-start(f32[2,32,4096]{2,1,0:T(8,128)} %param.19) | copy-start | bytes 3145732
Sparse Core Ops, SparseCore 0:
  11.5 79.7 all-gather.12
  94.9 75.9 all-gather.14
  174.5 75.9 all-gather.16
  253.9 75.9 all-gather.22
  333.3 75.9 all-gather.20
  412.8 75.9 all-gather.18
  616.2 149.9 reduce-scatter.14
  768.4 148.8 reduce-scatter.16
  919.7 148.8 reduce-scatter.10
  1070.7 148.9 reduce-scatter.12
  1221.9 148.8 reduce-scatter.6
  1373.0 148.8 reduce-scatter.8
where the time goes:
time: 1590 us; the launch traced here: 1580 us
  waiting for transfers between devices  1050 us (66%)
  matrix products  428 us (27%)
  blocking collectives  36.9 us (2%)
  local copies, waits for them, and re-layouts  21.9 us (1%)
  other arithmetic  20.6 us (1%)
  between operations  17.4 us (1%)
    reduce_scatter x6, waiting for transfers between devices, step(): lax.psum_scatter(by_w[name], 'dp', scatter_dimension=0, tiled=True)  732 us
    all_gather x6, waiting for transfers between devices, fetched(): lax.all_gather(w[number], 'dp', axis=0, tiled=True)  320 us
    dot_general x5, matrix products, layer(): gate = jnp.dot(a, w['w_gate'], preferred_element_type=jnp.float32)  156 us
    dot_general x5, matrix products, layer(): up = jnp.dot(a, w['w_up'], preferred_element_type=jnp.float32)  144 us
    dot_general x5, matrix products, matmul(): jnp.dot(a, w, preferred_element_type=jnp.float32).astype(jnp.bfloat16)  128 us
    psum x1, blocking collectives, step(): squares = lax.psum(sum((jnp.sum(g * g) for g in gradients)), 'dp')  36.9 us
  transfers between devices with their start and end apart: 12, of which 11 were waited for; matrix products, arithmetic and copies ran while one was open for 21% of the time, Pallas kernels for 0%

commit v1 on v0

v1 whole, which is shorter than its diff:
```python
import functools

import jax
import jax.numpy as jnp
from jax import lax
from jax.experimental import pallas as pl
from jax.experimental.pallas import tpu as pltpu
from jax.sharding import PartitionSpec as P

NAMES = ("w_gate", "w_up", "w_down")
BF, F32 = jnp.bfloat16, jnp.float32
MESH = pl.DeviceIdType.MESH
CHUNKS = 24
SLOTS = 8


def matmul(a, w):
    return jnp.dot(a, w, preferred_element_type=jnp.float32).astype(jnp.bfloat16)


def normed(h):
    wide = h.astype(jnp.float32)
    scale = lax.rsqrt(jnp.mean(wide**2, -1, keepdims=True) + 1e-6)
    return (wide * scale).astype(jnp.bfloat16)


def layer(h, w):
    a = normed(h)
    gate = jnp.dot(a, w["w_gate"], preferred_element_type=jnp.float32)
    up = jnp.dot(a, w["w_up"], preferred_element_type=jnp.float32)
    return h + matmul((jax.nn.silu(gate) * up).astype(jnp.bfloat16), w["w_down"])


def adamw(w, m, v, g):
    m = 0.9 * m + 0.1 * g
    v = 0.95 * v + 0.05 * g * g
    step = m * lax.rsqrt(v + 1e-8) + 0.1 * w
    return (w - 0.02 * step).astype(jnp.bfloat16), m, v


def place():
    me = lax.axis_index("dp")
    return me // 16, (me // 8) % 2, (me // 2) % 4, me % 2


def number(x, y, z, c):
    return ((x * 2 + y) * 4 + z) * 2 + c


def greet():
    x, y, z, c = place()
    barrier = pltpu.get_barrier_semaphore()
    others = [(1 - x, y, z, c), (x, 1 - y, z, c), (x, y, z, 1 - c)]
    others += [(x, y, (z + hop) % 4, c) for hop in (1, 2, 3)]
    for other in others:
        pl.semaphore_signal(barrier, 1, device_id={"dp": number(*other)}, device_id_type=MESH)
    pl.semaphore_wait(barrier, len(others))


def send(src, dst, sems, where):
    return pltpu.make_async_remote_copy(
        src_ref=src, dst_ref=dst, send_sem=sems[0], recv_sem=sems[1], device_id={"dp": number(*where)}, device_id_type=MESH
    )


def gather_chunks():
    order = []
    for layer_number in range(2):
        first = 3 * layer_number
        order += [(first + i, 1024 * q, 1024) for q in range(4) for i in (0, 1)]
        order += [(first + 2, 256 * q, 256) for q in range(4)]
    return order


GATHER_AT = (0, 2, 4, 6, 8)


def gather_kernel(*refs):
    shards, whole = refs[0:6], refs[6:12]
    mine, sems, local = refs[12:18], refs[18], refs[19]
    x, y, z, c = place()
    for i in range(6):
        pltpu.make_async_copy(shards[i], mine[i], local.at[i]).start()
    greet()
    chunks = gather_chunks()

    def copies(k, stage):
        i, first, columns = chunks[k]
        cut = pl.ds(first, columns)
        full = whole[i]

        def pair(n):
            return sems.at[0, k, n], sems.at[1, k, n]

        near = (x, 1 - y, z, c) if k % 2 == 0 else (1 - x, y, z, c)
        far = (1 - x, y, z, c) if k % 2 == 0 else (x, 1 - y, z, c)
        twin = (x, y, z, 1 - c)
        if stage == 0:
            own = full.at[x, y, z, c, :, cut]
            return [lambda hop=hop: send(shards[i].at[:, cut], own, pair(hop - 1), (x, y, (z + hop) % 4, c)) for hop in (1, 2, 3)]
        if stage == 1:
            part = full.at[x, y, :, c, :, cut]
            return [lambda: send(part, part, pair(3), near), lambda: send(part, part, pair(4), twin)]
        if stage == 2:
            part = full.at[x, :, :, c, :, cut] if k % 2 == 0 else full.at[:, y, :, c, :, cut]
            late = full.at[x, 1 - y, :, c, :, cut] if k % 2 == 0 else full.at[1 - x, y, :, c, :, cut]
            return [lambda: send(part, part, pair(5), far), lambda: send(late, late, pair(6), twin)]
        part = full.at[1 - x, :, :, c, :, cut] if k % 2 == 0 else full.at[:, 1 - y, :, c, :, cut]
        return [lambda: send(part, part, pair(7), twin)]

    for i in range(6):
        pltpu.make_async_copy(shards[i], mine[i], local.at[i]).wait()
        pltpu.make_async_copy(mine[i], whole[i].at[x, y, z, c], local.at[i]).start()
    for t in range(CHUNKS + GATHER_AT[-1]):
        if t == 2:
            for i in range(6):
                pltpu.make_async_copy(mine[i], whole[i].at[x, y, z, c], local.at[i]).wait()
        for stage in (4, 3, 2, 1, 0):
            k = t - GATHER_AT[stage]
            if not 0 <= k < CHUNKS:
                continue
            if stage in (1, 2, 3):
                for copy in copies(k, stage - 1)[: 3 if stage == 1 else 1]:
                    copy().wait_recv()
            if stage == 4:
                for copy in copies(k, 1)[1:] + copies(k, 2)[1:] + copies(k, 3):
                    copy().wait_recv()
                for past in range(4):
                    for copy in copies(k, past):
                        copy().wait_send()
            else:
                for copy in copies(k, stage):
                    copy().start()


def gathered(weights):
    shards = [w[n] for n in range(2) for w in weights]
    tall = [s.shape for s in shards]
    return pl.pallas_call(
        gather_kernel,
        name="gather",
        out_shape=[jax.ShapeDtypeStruct((2, 2, 4, 2) + s, BF) for s in tall],
        in_specs=[pl.BlockSpec(memory_space=pl.ANY)] * 6,
        out_specs=[pl.BlockSpec(memory_space=pl.ANY)] * 6,
        scratch_shapes=[pltpu.VMEM(s, BF) for s in tall]
        + [pltpu.SemaphoreType.DMA((2, CHUNKS, 8)), pltpu.SemaphoreType.DMA((6,))],
        compiler_params=pltpu.CompilerParams(collective_id=0, has_side_effects=True),
    )(*shards)


SUM_AT = (0, 1, 3, 5, 6)


def wide(ref, *at):
    return ref[at].astype(F32)


def sum_stages(k, own, fromtwin, fromfar, fromnear, fromz, sems, out, squares):
    x, y, z, c = place()
    slot, color = k % SLOTS, k % 2
    f, n = x + color * (y - x), y + color * (x - y)
    far = (x + (1 - color) * (1 - 2 * x), y + color * (1 - 2 * y), z, c)
    near = (x + color * (1 - 2 * x), y + (1 - color) * (1 - 2 * y), z, c)

    def pair(i):
        return sems.at[0, slot, i], sems.at[1, slot, i]

    def to_twin():
        return send(own.at[SLOTS + k % 2], fromtwin.at[slot], pair(0), (x, y, z, 1 - c))

    def to_far():
        return send(fromtwin.at[slot, pl.ds((1 - f) * 8, 8)], fromfar.at[slot], pair(1), far)

    def to_near():
        return send(fromtwin.at[slot, pl.ds(f * 8 + (1 - n) * 4, 4)], fromnear.at[slot], pair(2), near)

    base = f * 8 + n * 4

    def to_z(hop):
        to = (z + hop) % 4
        return send(fromtwin.at[slot, base + to], fromz.at[slot, hop - 1], pair(2 + hop), (x, y, to, c))

    def first():
        to_twin().start()

    def second():
        to_twin().wait()

        def add(i, _):
            p = (1 - f) * 8 + i
            fromtwin[slot, p] = (wide(own, slot, p) + wide(fromtwin, slot, p)).astype(BF)
            return 0

        lax.fori_loop(0, 8, add, 0)
        to_far().start()

    def third():
        to_far().wait_recv()

        def add(i, _):
            q = (1 - n) * 4 + i
            p = f * 8 + q
            fromtwin[slot, p] = (wide(own, slot, p) + wide(fromtwin, slot, p) + wide(fromfar, slot, q)).astype(BF)
            return 0

        lax.fori_loop(0, 4, add, 0)
        to_near().start()

    def fourth():
        to_near().wait_recv()
        for hop in (1, 2, 3):
            to = (z + hop) % 4
            p, q = base + to, n * 4 + to
            total = wide(own, slot, p) + wide(fromtwin, slot, p) + wide(fromfar, slot, q) + wide(fromnear, slot, to)
            fromtwin[slot, p] = total.astype(BF)
            to_z(hop).start()

    def fifth():
        for hop in (1, 2, 3):
            to_z(hop).wait()
        to_far().wait_send()
        to_near().wait_send()
        p, q = base + z, n * 4 + z
        total = wide(own, slot, p) + wide(fromtwin, slot, p) + wide(fromfar, slot, q) + wide(fromnear, slot, z)
        total = (total + wide(fromz, slot, 0) + wide(fromz, slot, 1) + wide(fromz, slot, 2)).astype(BF)
        out[k] = total
        square = total.astype(F32)
        square = square * square
        squares[...] += jnp.sum(square.reshape(16, 8, 256), axis=0)

    return first, second, third, fourth, fifth


def sum_tick(t, bufs):
    for stage in (4, 3, 2, 1, 0):
        k = t - SUM_AT[stage]

        @pl.when(jnp.logical_and(k >= 0, k < CHUNKS))
        def _():
            sum_stages(k, *bufs)[stage]()


def all_squares(squares, total, box, sems):
    x, y, z, c = place()
    box[0] = jnp.broadcast_to(jnp.sum(squares[...]), (8, 128))
    for i, other in enumerate([(x, y, z, 1 - c), (1 - x, y, z, c), (x, 1 - y, z, c)]):
        copy = send(box.at[i], box.at[7 + i], (sems.at[0, i], sems.at[1, i]), other)
        copy.start()
        copy.wait()
        box[i + 1] = box[i] + box[7 + i]
    copies = [
        send(box.at[3], box.at[3 + hop], (sems.at[0, 2 + hop], sems.at[1, 2 + hop]), (x, y, (z + hop) % 4, c)) for hop in (1, 2, 3)
    ]
    for copy in copies:
        copy.start()
    for copy in copies:
        copy.wait()
    total[...] = (box[3] + box[5]) + (box[4] + box[6])


def sum_kernel(dg, du, dd, out, total, own, fromtwin, fromfar, fromnear, fromz, squares, box, sems, last, load):
    x, y, z, c = place()
    squares[...] = jnp.zeros_like(squares)
    greet()
    bufs = (own, fromtwin, fromfar, fromnear, fromz, sems, out, squares)

    def tick(t, _):
        @pl.when(t < CHUNKS)
        def _():
            lay, r = 1 - t // 12, t % 12
            color = t % 2

            def fill(go):
                for b in range(4):
                    bx, by = b // 2, b % 2
                    spot = bx * 8 + by * 4 + color * (by * 8 + bx * 4 - bx * 8 - by * 4)
                    for rail in range(2):
                        same = 1 - (rail - c) * (rail - c)
                        s = same * (t % SLOTS) + (1 - same) * (SLOTS + t % 2)
                        for j in range(4):
                            dst = own.at[s, pl.ds(spot, 4), j]
                            q = r // 2

                            @pl.when(jnp.logical_and(r < 8, r % 2 == 0))
                            def _():
                                cp = pltpu.make_async_copy(dg.at[lay, bx, by, :, rail, :, pl.ds(q * 1024 + j * 256, 256)], dst, load.at[b, rail, j])
                                go(cp)

                            @pl.when(jnp.logical_and(r < 8, r % 2 == 1))
                            def _():
                                cp = pltpu.make_async_copy(du.at[lay, bx, by, :, rail, :, pl.ds(q * 1024 + j * 256, 256)], dst, load.at[b, rail, j])
                                go(cp)

                            @pl.when(r >= 8)
                            def _():
                                cp = pltpu.make_async_copy(
                                    dd.at[lay, bx, by, :, rail, pl.ds(32 * j, 32), pl.ds((r - 8) * 256, 256)], dst, load.at[b, rail, j]
                                )
                                go(cp)

            fill(lambda cp: cp.start())
            fill(lambda cp: cp.wait())

        sum_tick(t, bufs)
        return 0

    lax.fori_loop(0, CHUNKS + SUM_AT[-1], tick, 0)
    all_squares(squares, total, box, last)


def summed(dg, du, dd):
    block = (4, 32, 256)
    return pl.pallas_call(
        sum_kernel,
        name="summed",
        out_shape=[jax.ShapeDtypeStruct((CHUNKS,) + block, BF), jax.ShapeDtypeStruct((8, 128), F32)],
        in_specs=[pl.BlockSpec(memory_space=pl.ANY)] * 3,
        out_specs=[pl.BlockSpec(memory_space=pltpu.VMEM)] * 2,
        scratch_shapes=[
            pltpu.VMEM((SLOTS + 2, 16) + block, BF),
            pltpu.VMEM((SLOTS, 16) + block, BF),
            pltpu.VMEM((SLOTS, 8) + block, BF),
            pltpu.VMEM((SLOTS, 4) + block, BF),
            pltpu.VMEM((SLOTS, 3) + block, BF),
            pltpu.VMEM((8, 256), F32),
            pltpu.VMEM((10, 8, 128), F32),
            pltpu.SemaphoreType.DMA((2, SLOTS, 6)),
            pltpu.SemaphoreType.DMA((2, 6)),
            pltpu.SemaphoreType.DMA((4, 2, 4)),
        ],
        compiler_params=pltpu.CompilerParams(collective_id=1, has_side_effects=True, vmem_limit_bytes=48 * 2**20),
    )(dg, du, dd)


def solution(mesh):
    def step(x, dy, *arrays):
        weights, m, v = (arrays[i : i + 3] for i in (0, 3, 6))
        full = [w.reshape(-1, w.shape[-1]) for w in gathered(weights)]
        whole = [dict(zip(NAMES, full[3 * n : 3 * n + 3], strict=True)) for n in range(2)]
        h0, by_h = x[0], dy[0]
        h1 = layer(h0, whole[0])
        grads = [None, None]
        for n, h in ((1, h1), (0, h0)):
            _, back = jax.vjp(lambda w, h: layer(h, w), whole[n], h)
            grads[n], by_h = back(by_h)
        dg, du, dd = (jnp.stack([grads[n][name].reshape(2, 2, 4, 2, -1, grads[n][name].shape[-1]) for n in range(2)]) for name in NAMES)
        sums, squares = summed(dg, du, dd)
        sums = sums.reshape(2, 12, 4, 32, 256)[::-1]
        mine = []
        for i in range(2):
            mine.append(sums[:, i:8:2].transpose(0, 3, 1, 2, 4).reshape(2, 32, 4096))
        mine.append(sums[:, 8:].transpose(0, 2, 3, 1, 4).reshape(2, 128, 1024))
        count = 32 * sum(g.size for g in mine)
        factor = jnp.minimum(1.0, 0.5 * lax.rsqrt(squares[0, 0] / count + 1e-30))
        new = [adamw(w.astype(F32), m, v, g.astype(F32) * factor) for w, m, v, g in zip(weights, m, v, mine, strict=True)]
        return tuple(one[which] for which in range(3) for one in new)

    states, cut = P(("rep", "dp"), None, None), P(None, "dp", None)
    return jax.shard_map(
        step,
        mesh=mesh,
        in_specs=(states, states) + (cut,) * 9,
        out_specs=(P("rep", "dp", None),) * 9,
        check_vma=False,
    )
```

time: 1590 us -> 977 us (0.61)
  waiting for transfers between devices: 1050 us -> 0 us
  Pallas kernels: 0 us -> 470 us
  blocking collectives: 36.9 us -> 0 us
  other arithmetic: 20.6 us -> 52.7 us
    reduce_scatter x6 -> x0, waiting for transfers between devices: 732 us -> none  [step(): lax.psum_scatter(by_w[name], 'dp', scatter_dimension=0, tiled=True)]
    pallas_call x0 -> x2, Pallas kernels: none -> 470 us  [the longest x1 243 us: summed(): pl.pallas_call(sum_kernel, name='summed', out_shape=[jax.ShapeDtypeStruct...]
    all_gather x6 -> x0, waiting for transfers between devices: 320 us -> none  [fetched(): lax.all_gather(w[number], 'dp', axis=0, tiled=True)]
    psum x1 -> x0, blocking collectives: 36.9 us -> none  [step(): squares = lax.psum(sum((jnp.sum(g * g) for g in gradients)), 'dp')]
    another operation x0 -> x3, other arithmetic: none -> 31.1 us  [step(): jnp.stack([grads[n][name].reshape(2, 2, 4, 2, -1, grads[n][name].shape[-1...]
  transfers between devices with their start and end apart: 12 -> 0, of which waited for: 11 -> 0; matrix products, arithmetic and copies ran while one was open for 21% -> 0% of each run, Pallas kernels for 0% -> 0%
where the time goes in v1:
time: 977 us; the launch traced here: 971 us
  Pallas kernels  470 us (48%)
  matrix products  424 us (43%)
  other arithmetic  52.7 us (5%)
  local copies, waits for them, and re-layouts  22.6 us (2%)
    pallas_call x1, Pallas kernels, summed(): pl.pallas_call(sum_kernel, name='summed', out_shape=[jax.ShapeDtypeStruct...  243 us
    pallas_call x1, Pallas kernels, gathered(): pl.pallas_call(gather_kernel, name='gather', out_shape=[jax.ShapeDtypeStr...  226 us
    dot_general x5, matrix products, layer(): gate = jnp.dot(a, w['w_gate'], preferred_element_type=jnp.float32)  154 us
    dot_general x5, matrix products, layer(): up = jnp.dot(a, w['w_up'], preferred_element_type=jnp.float32)  142 us
    dot_general x5, matrix products, matmul(): jnp.dot(a, w, preferred_element_type=jnp.float32).astype(jnp.bfloat16)  128 us
    another operation x3, other arithmetic, step(): jnp.stack([grads[n][name].reshape(2, 2, 4, 2, -1, grads[n][name].shape[-1...  31.1 us

profile of v1, /device:TPU:0, one launch (start us, length us, event | category | flops | bytes accessed | tf_op | source)
XLA Modules:
  0.0 971.0 jit_solution(1574841871514056242)
XLA Ops:
  0.6 2.2 slice_bitcast_fusion.1
  2.8 1.9 slice_bitcast_fusion
  4.7 226.4 %gather.1 = (bf16[2,2,4,2,32,4096]{5,4,3,2,1,0:T(8,128)(2,1)}, bf16[2,2,4,2,32,4096]{5,4,3,2,1,0:T(8,128)(2,1)}, bf16[2,2,4,2,128,1024]{5,4,3,2,1,0:T(8,128)(2,1...) custom-call(bf16[32,4096]{1,0:T(8,128)(2,1)} %get-tuple-element.51.r, ...), custom_call_target="tpu_custom_call" | custom-call | tf_op jit(solution)/shard_map/gather/pallas_call | solution.py:139
  231.1 6.7 copy.20
  237.8 3.1 fusion.15
  240.9 24.4 %fusion.43 = f32[2048,4096]{1,0:T(8,128)} fusion(bf16[1024,4096]{1,0:T(8,128)(2,1)} %bitcast.95, bf16[1,2048,1024]{2,1,0:T(8,128)(2,1)} %param.11, f32[2048]{0:T(1024)S(1)} %add_rsqrt_fusion), kind=kOutput, calls=%fused_computation.59 | convolution fusion | flops 17186160640 | bytes 46145536 | tf_op jit(solution)/shard_map/dot_general | solution.py:29
  265.3 35.9 %multiply_convert_fusion.1 = (bf16[2048,4096]{1,0:T(8,128)(2,1)}, f32[2048,4096]{1,0:T(8,128)}) fusion(f32[2048,4096]{1,0:T(8,128)} %fusion.43, bf16[1024,4096]{1,0:T(8,128)(2,1)} %bitcast.94, bf16[1,2048,1024]{2,1,0:T(8,128)(2,1)} %param.11, f32[2048]{0:T(1024)S(1)} %add_rsqrt_fusion), kind=kOutput, calls=%fused_computation.17 | convolution fusion | flops 17236492288 | bytes 96477184 | tf_op jit(solution)/shard_map/dot_general | solution.py:30
  301.2 23.8 %fusion.19 = (f32[2048]{0:T(1024)S(1)}, bf16[2048,1024]{0,1:T(8,128)(2,1)S(1)}) fusion(bf16[2048,4096]{1,0:T(8,128)(2,1)} %get-tuple-element.43, bf16[4096,1024]{1,0:T(8,128)(2,1)} %bitcast.87, bf16[1,2048,1024]{1,2,0:T(8,128)(2,1)} %copy.20), kind=kOutput, calls=%fused_computation.40 | convolution fusion | flops 17190352896 | bytes 33562624 | tf_op jit(solution)/shard_map/dot_general | solution.py:18
  325.0 0.0 copy-start.1
  325.0 0.0 copy-start.11
  325.0 0.0 copy-start.9
  325.0 0.0 copy-start.4
  325.1 24.9 %fusion.37 = f32[2048,4096]{1,0:T(8,128)} fusion(bf16[1024,4096]{1,0:T(8,128)(2,1)} %bitcast.89, bf16[2048,1024]{0,1:T(8,128)(2,1)S(1)} %get-tuple-element.46, f32[2048]{0:T(1024)S(1)} %fusion.57), kind=kOutput, calls=%fused_computation.56 | convolution fusion | flops 17186160640 | bytes 46145536 | tf_op jit(solution)/shard_map/jvp()/dot_general | solution.py:30
  349.9 23.9 %convolution_convert_fusion.1 = bf16[4096,2048]{0,1:T(8,128)(2,1)} fusion(bf16[4096,1024]{1,0:T(8,128)(2,1)} %bitcast.93, bf16[1,2048,1024]{2,1,0:T(8,128)(2,1)S(1)} %copy-done.4), kind=kOutput, calls=%fused_computation.28 | convolution fusion | flops 17188257792 | bytes 29360128 | tf_op jit(solution)/shard_map/transpose(jvp())/dot_general | solution.py:18
  373.9 46.6 %fusion.2 = (bf16[2048,4096]{1,0:T(8,128)(2,1)}, f32[2048,4096]{1,0:T(8,128)}) fusion(f32[2048,4096]{1,0:T(8,128)} %fusion.37, bf16[4096,2048]{0,1:T(8,128)(2,1)} %convolution_convert_fusion.1, bf16[1024,4096]{1,0:T(8,128)(2,1)} %bitcast.91, bf16[2048,1024]{0,1:T(8,128)(2,1)} %copy-done.1, f32[2048]{0:T(1024)S(1)} %fusion.57), kind=kOutput, calls=%fused_computation.6 | convolution fusion | flops 17286823936 | bytes 113254400 | tf_op jit(solution)/shard_map/jvp()/dot_general | solution.py:29
  420.5 24.1 %fusion.67 = bf16[2048,1024]{0,1:T(8,128)(2,1)} fusion(bf16[2048,4096]{1,0:T(8,128)(2,1)} %get-tuple-element.47, bf16[1024,4096]{1,0:T(8,128)(2,1)} %bitcast.92), kind=kOutput, calls=%fused_computation.100 | convolution fusion | flops 17179869184 | bytes 29360128 | tf_op jit(solution)/shard_map/transpose(jvp())/dot_general | solution.py:29
  444.6 30.2 %fusion.21 = (f32[2048]{0:T(1024)S(1)}, bf16[2048,1024]{0,1:T(8,128)(2,1)}) fusion(bf16[2048,1024]{0,1:T(8,128)(2,1)S(1)} %copy-done.2, bf16[2048,1024]{0,1:T(8,128)(2,1)} %fusion.67, bf16[1024,4096]{1,0:T(8,128)(2,1)} %bitcast.90, bf16[4096,2048]{0,1:T(8,128)(2,1)} %convolution_convert_fusion.1, f32[2048,4096]{1,0:T(8,128)} %get-tuple-element.48), kind=kOutput, calls=%fused_computation.42 | convolution fusion | flops 17242781696 | bytes 71311360 | tf_op jit(solution)/shard_map/transpose(jvp())/dot_general | solution.py:30
  474.8 6.5 copy.21
  481.3 6.2 fusion.30
  487.5 0.0 copy-start.5
  487.5 24.8 %convolution_convert_fusion.2 = bf16[4096,1024]{1,0:T(8,128)(2,1)} fusion(bf16[2048,4096]{1,0:T(8,128)(2,1)} %get-tuple-element.43, bf16[2048,1024]{0,1:T(8,128)(2,1)S(1)} %fusion.30), kind=kOutput, calls=%fused_computation.48 | convolution fusion | flops 17184063488 | bytes 29360128 | tf_op jit(solution)/shard_map/transpose(jvp())/dot_general | solution.py:18
  512.4 29.9 %fusion.25 = bf16[4096,1024]{1,0:T(8,128)(2,1)} fusion(f32[2048,4096]{1,0:T(8,128)} %fusion.37, bf16[1,2048,1024]{2,1,0:T(8,128)(2,1)S(1)} %copy-done.5, f32[2048,4096]{1,0:T(8,128)} %get-tuple-element.48), kind=kOutput, calls=%fused_computation.45 | convolution fusion | flops 17234395136 | bytes 79691776 | tf_op jit(solution)/shard_map/transpose(jvp())/dot_general | solution.py:18
  542.3 13.8 %pad_maximum_fusion.2.dd = bf16[2,2,2,4,2,128,1024]{6,5,4,3,2,1,0:T(8,128)(2,1)} fusion(bf16[1,2,2,4,2,128,1024]{6,5,4,3,2,1,0:T(8,128)(2,1)} %bitcast.86, bf16[1,2,2,4,2,128,1024]{6,5,4,3,2,1,0:T(8,128)(2,1)} %bitcast.83), kind=kLoop, calls=%fused_computation.25 | loop fusion | flops 8388608 | bytes 33554432 | tf_op jit(solution)/shard_map/stack | solution.py:346
  556.2 25.1 %convolution_convert_fusion = bf16[2048,4096]{1,0:T(8,128)(2,1)} fusion(bf16[2048,1024]{0,1:T(8,128)(2,1)} %copy-done.3, bf16[4096,1024]{1,0:T(8,128)(2,1)} %bitcast.88), kind=kOutput, calls=%fused_computation.27 | convolution fusion | flops 17188257792 | bytes 29360128 | tf_op jit(solution)/shard_map/transpose(jvp())/dot_general | solution.py:18
  581.3 24.7 %fusion.27 = bf16[1024,4096]{1,0:T(8,128)(2,1)S(1)} fusion(bf16[2048,4096]{1,0:T(8,128)(2,1)} %convolution_convert_fusion, f32[2048,4096]{1,0:T(8,128)} %fusion.43, bf16[1,2048,1024]{1,2,0:T(8,128)(2,1)} %copy.20, f32[2048]{0:T(1024)S(1)} %copy-done.14), kind=kOutput, calls=%fused_computation.47 | convolution fusion | flops 17240686592 | bytes 62922752 | tf_op jit(solution)/shard_map/transpose(jvp())/dot_general | solution.py:30
  606.0 26.7 %fusion.26 = bf16[1024,4096]{1,0:T(8,128)(2,1)} fusion(bf16[4096,2048]{0,1:T(8,128)(2,1)} %convolution_convert_fusion.1, bf16[2048,1024]{0,1:T(8,128)(2,1)} %copy-done.1, f32[2048]{0:T(1024)S(1)} %copy-done.10, f32[2048,4096]{1,0:T(8,128)} %get-tuple-element.48), kind=kOutput, calls=%fused_computation.46 | convolution fusion | flops 17240686592 | bytes 62922752 | tf_op jit(solution)/shard_map/transpose(jvp())/dot_general | solution.py:30
  632.7 10.5 %pad_maximum_fusion.1.du = bf16[2,2,2,4,2,32,4096]{6,5,4,3,2,1,0:T(8,128)(2,1)} fusion(bf16[1,2,2,4,2,32,4096]{6,5,4,3,2,1,0:T(8,128)(2,1)} %bitcast.85, bf16[1,2,2,4,2,32,4096]{6,5,4,3,2,1,0:T(8,128)(2,1)S(1)} %bitcast.84), kind=kLoop, calls=%fused_computation.24 | loop fusion | flops 8388608 | bytes 33554432 | tf_op jit(solution)/shard_map/stack | solution.py:346
  643.2 37.1 %fusion.22 = bf16[1024,4096]{1,0:T(8,128)(2,1)} fusion(f32[2048,4096]{1,0:T(8,128)} %fusion.43, f32[2048,4096]{1,0:T(8,128)} %get-tuple-element.44, bf16[2048,4096]{1,0:T(8,128)(2,1)} %convolution_convert_fusion, bf16[1,2048,1024]{1,2,0:T(8,128)(2,1)} %copy.20, f32[2048]{0:T(1024)S(1)} %copy-done.14), kind=kOutput, calls=%fused_computation.44 | convolution fusion | flops 17282629632 | bytes 96477184 | tf_op jit(solution)/shard_map/transpose(jvp())/dot_general | solution.py:29
  680.4 21.6 %convolution_convert_fusion.3 = bf16[1024,4096]{1,0:T(8,128)(2,1)S(1)} fusion(bf16[2048,4096]{1,0:T(8,128)(2,1)} %get-tuple-element.47, bf16[2048,1024]{0,1:T(8,128)(2,1)} %copy-done.1, f32[2048]{0:T(1024)S(1)} %copy-done.10), kind=kOutput, calls=%fused_computation.49 | convolution fusion | flops 17186160640 | bytes 29368320 | tf_op jit(solution)/shard_map/transpose(jvp())/dot_general | solution.py:29
  702.0 6.8 pad_maximum_fusion.dg
  708.8 243.5 %summed.1 = (bf16[24,4,32,256]{3,2,1,0:T(8,128)(2,1)S(1)}, f32[8,128]{1,0:T(8,128)S(1)}) custom-call(bf16[2,2,2,4,2,32,4096]{6,5,4,3,2,1,0:T(8,128)(2,1)} %pad_maximum_fusion.dg, bf16[2,2,2,4,2,32,4096]{6,5,4,3,2,1,0:T(8,128)(2,1)} %pad_maximum_fusion.1.du, bf16[2,2,2,4,2,128,1024]{6,5,4,3,2,1,0:T(8,128)(2,1)} %pad_maximum_fusion.2.dd), custom_call_target="tpu_custom_call" | custom-call | tf_op jit(solution)/shard_map/summed/pallas_call | solution.py:313
  952.3 0.0 copy-start.6
  952.3 1.1 fusion.66
  953.4 0.5 slice.47
  954.6 0.1 multiply_bitcast_fusion
  954.8 0.0 copy-start.7
  954.8 0.7 copy.25
  955.5 0.5 mul.291
  956.0 3.3 fusion.53
  959.4 1.2 multiply_bitcast_fusion.1
  960.5 0.0 copy-start.8
  960.5 0.7 copy.24
  961.2 0.5 mul.279
  961.8 3.3 fusion.50
  965.0 1.2 multiply_bitcast_fusion.2
  966.2 0.7 copy.23
  966.9 0.5 mul.268
  967.5 3.3 fusion.47
  (25 shorter events, 0.1 us)
Async XLA Ops:
  240.9 24.5 %copy-start.13 = (f32[2048]{0:T(1024)}, f32[2048]{0:T(1024)S(1)}, u32[]{:S(2)}) copy-start(f32[2048]{0:T(1024)S(1)} %add_rsqrt_fusion) | copy-start | bytes 24580
  325.0 24.9 %copy-start.1 = (bf16[2048,1024]{0,1:T(8,128)(2,1)}, bf16[2048,1024]{0,1:T(8,128)(2,1)S(1)}, u32[]{:S(2)}) copy-start(bf16[2048,1024]{0,1:T(8,128)(2,1)S(1)} %get-tuple-element.46) | copy-start | bytes 12582916
  325.0 24.9 %copy-start.11 = (f32[2048]{0:T(1024)}, f32[2048]{0:T(1024)S(1)}, u32[]{:S(2)}) copy-start(f32[2048]{0:T(1024)S(1)} %get-tuple-element.45) | copy-start | bytes 24580
  325.0 156.3 %copy-start.9 = (f32[2048]{0:T(1024)}, f32[2048]{0:T(1024)S(1)}, u32[]{:S(2)}) copy-start(f32[2048]{0:T(1024)S(1)} %fusion.57) | copy-start | bytes 24580
  325.0 24.9 %copy-start.4 = (bf16[1,2048,1024]{2,1,0:T(8,128)(2,1)S(1)}, bf16[1,2048,1024]{2,1,0:T(8,128)(2,1)}, u32[]{:S(2)}) copy-start(bf16[1,2048,1024]{2,1,0:T(8,128)(2,1)} %param.12) | copy-start | bytes 12582916
  420.4 24.1 %copy-start.2 = (bf16[2048,1024]{0,1:T(8,128)(2,1)S(1)}, bf16[2048,1024]{0,1:T(8,128)(2,1)}, u32[]{:S(2)}) copy-start(bf16[2048,1024]{0,1:T(8,128)(2,1)} %copy-done.1) | copy-start | bytes 12582916
  444.6 30.2 %copy-start.12 = (f32[2048]{0:T(1024)S(1)}, f32[2048]{0:T(1024)}, u32[]{:S(2)}) copy-start(f32[2048]{0:T(1024)} %copy-done.11) | copy-start | bytes 24580
  487.5 24.9 %copy-start.3 = (bf16[2048,1024]{0,1:T(8,128)(2,1)}, bf16[2048,1024]{0,1:T(8,128)(2,1)S(1)}, u32[]{:S(2)}) copy-start(bf16[2048,1024]{0,1:T(8,128)(2,1)S(1)} %fusion.30) | copy-start | bytes 12582916
  487.5 24.9 %copy-start.5 = (bf16[1,2048,1024]{2,1,0:T(8,128)(2,1)S(1)}, bf16[1,2048,1024]{2,1,0:T(8,128)(2,1)}, u32[]{:S(2)}) copy-start(bf16[1,2048,1024]{2,1,0:T(8,128)(2,1)} %param.12) | copy-start | bytes 12582916
  556.1 25.2 %copy-start.14 = (f32[2048]{0:T(1024)S(1)}, f32[2048]{0:T(1024)}, u32[]{:S(2)}) copy-start(f32[2048]{0:T(1024)} %copy-done.13) | copy-start | bytes 24580
  581.3 24.7 %copy-start.10 = (f32[2048]{0:T(1024)S(1)}, f32[2048]{0:T(1024)}, u32[]{:S(2)}) copy-start(f32[2048]{0:T(1024)} %copy-done.9) | copy-start | bytes 24580
  680.4 21.7 %copy-start = (bf16[1024,4096]{1,0:T(8,128)(2,1)S(1)}, bf16[1024,4096]{1,0:T(8,128)(2,1)}, u32[]{:S(2)}) copy-start(bf16[1024,4096]{1,0:T(8,128)(2,1)} %fusion.22) | copy-start | bytes 25165828
  952.3 3.7 copy-start.6
  954.8 7.0 copy-start.7
  960.5 6.9 copy-start.8

commit v2 on v1

v2 whole, which is shorter than its diff:
```python
import jax
import jax.numpy as jnp
from jax import lax
from jax.experimental import pallas as pl
from jax.experimental.pallas import tpu as pltpu
from jax.sharding import PartitionSpec as P

BF, F32 = jnp.bfloat16, jnp.float32
MESH = pl.DeviceIdType.MESH
CHUNKS = 24
SLOTS, OWN, OTHER = 6, 7, 3


def adamw(w, m, v, g):
    m = 0.9 * m + 0.1 * g
    v = 0.95 * v + 0.05 * g * g
    step = m * lax.rsqrt(v + 1e-8) + 0.1 * w
    return (w - 0.02 * step).astype(jnp.bfloat16), m, v


def place():
    me = lax.axis_index("dp")
    return me // 16, (me // 8) % 2, (me // 2) % 4, me % 2


def number(x, y, z, c):
    return ((x * 2 + y) * 4 + z) * 2 + c


def greet():
    x, y, z, c = place()
    barrier = pltpu.get_barrier_semaphore()
    others = [(1 - x, y, z, c), (x, 1 - y, z, c), (x, y, z, 1 - c)]
    others += [(x, y, (z + hop) % 4, c) for hop in (1, 2, 3)]
    for other in others:
        pl.semaphore_signal(barrier, 1, device_id={"dp": number(*other)}, device_id_type=MESH)
    pl.semaphore_wait(barrier, len(others))


def send(src, dst, sems, where):
    return pltpu.make_async_remote_copy(
        src_ref=src, dst_ref=dst, send_sem=sems[0], recv_sem=sems[1], device_id={"dp": number(*where)}, device_id_type=MESH
    )


def gather_chunks():
    wide = [[(3 * n + i, 1024 * q, 1024) for q in range(4) for i in (0, 1)] for n in range(2)]
    tall = [[(3 * n + 2, 256 * q, 256) for q in range(4)] for n in range(2)]
    return wide[0] + tall[0] + tall[1] + wide[1]


GATHER_AT = (0, 2, 4, 6, 8)


def gather_tick(t, shards, whole, sems):
    x, y, z, c = place()
    chunks = gather_chunks()

    def copies(k, stage):
        i, first, columns = chunks[k]
        cut = pl.ds(first, columns)
        full = whole[i]

        def pair(n):
            return sems.at[0, k, n], sems.at[1, k, n]

        near = (x, 1 - y, z, c) if k % 2 == 0 else (1 - x, y, z, c)
        far = (1 - x, y, z, c) if k % 2 == 0 else (x, 1 - y, z, c)
        twin = (x, y, z, 1 - c)
        if stage == 0:
            own = full.at[x, y, z, c, :, cut]
            return [lambda hop=hop: send(shards[i].at[:, cut], own, pair(hop - 1), (x, y, (z + hop) % 4, c)) for hop in (1, 2, 3)]
        if stage == 1:
            part = full.at[x, y, :, c, :, cut]
            return [lambda: send(part, part, pair(3), near), lambda: send(part, part, pair(4), twin)]
        if stage == 2:
            part = full.at[x, :, :, c, :, cut] if k % 2 == 0 else full.at[:, y, :, c, :, cut]
            late = full.at[x, 1 - y, :, c, :, cut] if k % 2 == 0 else full.at[1 - x, y, :, c, :, cut]
            return [lambda: send(part, part, pair(5), far), lambda: send(late, late, pair(6), twin)]
        part = full.at[1 - x, :, :, c, :, cut] if k % 2 == 0 else full.at[:, 1 - y, :, c, :, cut]
        return [lambda: send(part, part, pair(7), twin)]

    for stage in (4, 3, 2, 1, 0):
        k = t - GATHER_AT[stage]
        if not 0 <= k < CHUNKS:
            continue
        if stage in (1, 2, 3):
            for copy in copies(k, stage - 1)[: 3 if stage == 1 else 1]:
                copy().wait_recv()
        if stage == 4:
            for copy in copies(k, 1)[1:] + copies(k, 2)[1:] + copies(k, 3):
                copy().wait_recv()
            for past in range(4):
                for copy in copies(k, past):
                    copy().wait_send()
        else:
            for copy in copies(k, stage):
                copy().start()


SUM_AT = (0, 1, 3, 4, 5)


def wide(ref, *at):
    return ref[at].astype(F32)


def sum_stages(k, own, fromtwin, fromfar, fromnear, fromz, sems, out, squares):
    x, y, z, c = place()
    slot, mine, color = k % SLOTS, k % OWN, k % 2
    f, n = x + color * (y - x), y + color * (x - y)
    far = (x + (1 - color) * (1 - 2 * x), y + color * (1 - 2 * y), z, c)
    near = (x + color * (1 - 2 * x), y + (1 - color) * (1 - 2 * y), z, c)

    def pair(i):
        return sems.at[0, slot, i], sems.at[1, slot, i]

    def to_twin():
        return send(own.at[OWN + k % OTHER], fromtwin.at[slot], pair(0), (x, y, z, 1 - c))

    def to_far():
        return send(fromtwin.at[slot, pl.ds((1 - f) * 8, 8)], fromfar.at[slot], pair(1), far)

    def to_near():
        return send(fromtwin.at[slot, pl.ds(f * 8 + (1 - n) * 4, 4)], fromnear.at[slot], pair(2), near)

    base = f * 8 + n * 4

    def to_z(hop):
        to = (z + hop) % 4
        return send(fromtwin.at[slot, base + to], fromz.at[slot, hop - 1], pair(2 + hop), (x, y, to, c))

    def first():
        to_twin().start()

    def second():
        to_twin().wait()

        def add(i, _):
            p = (1 - f) * 8 + i
            fromtwin[slot, p] = (wide(own, mine, p) + wide(fromtwin, slot, p)).astype(BF)
            return 0

        lax.fori_loop(0, 8, add, 0)
        to_far().start()

    def third():
        to_far().wait_recv()

        def add(i, _):
            q = (1 - n) * 4 + i
            p = f * 8 + q
            fromtwin[slot, p] = (wide(own, mine, p) + wide(fromtwin, slot, p) + wide(fromfar, slot, q)).astype(BF)
            return 0

        lax.fori_loop(0, 4, add, 0)
        to_near().start()

    def fourth():
        to_near().wait_recv()
        for hop in (1, 2, 3):
            to = (z + hop) % 4
            p, q = base + to, n * 4 + to
            total = wide(own, mine, p) + wide(fromtwin, slot, p) + wide(fromfar, slot, q) + wide(fromnear, slot, to)
            fromtwin[slot, p] = total.astype(BF)
            to_z(hop).start()

    def fifth():
        for hop in (1, 2, 3):
            to_z(hop).wait()
        to_far().wait_send()
        to_near().wait_send()
        p, q = base + z, n * 4 + z
        total = wide(own, mine, p) + wide(fromtwin, slot, p) + wide(fromfar, slot, q) + wide(fromnear, slot, z)
        total = (total + wide(fromz, slot, 0) + wide(fromz, slot, 1) + wide(fromz, slot, 2)).astype(BF)
        out[k] = total
        square = total.astype(F32)
        square = square * square
        squares[...] += jnp.sum(square.reshape(16, 8, 256), axis=0)

    return first, second, third, fourth, fifth


def sum_tick(t, bufs):
    for stage in (4, 3, 2, 1, 0):
        k = t - SUM_AT[stage]

        @pl.when(jnp.logical_and(k >= 0, k < CHUNKS))
        def _():
            sum_stages(k, *bufs)[stage]()


def all_squares(squares, total, box, sems):
    x, y, z, c = place()
    box[0] = jnp.broadcast_to(jnp.sum(squares[...]), (8, 128))
    for i, other in enumerate([(x, y, z, 1 - c), (1 - x, y, z, c), (x, 1 - y, z, c)]):
        copy = send(box.at[i], box.at[7 + i], (sems.at[0, i], sems.at[1, i]), other)
        copy.start()
        copy.wait()
        box[i + 1] = box[i] + box[7 + i]
    copies = [
        send(box.at[3], box.at[3 + hop], (sems.at[0, 2 + hop], sems.at[1, 2 + hop]), (x, y, (z + hop) % 4, c)) for hop in (1, 2, 3)
    ]
    for copy in copies:
        copy.start()
    for copy in copies:
        copy.wait()
    total[...] = (box[3] + box[5]) + (box[4] + box[6])


NN, NT, TN = (((1,), (0,)), ((), ())), (((1,), (1,)), ((), ())), (((0,), (0,)), ((), ()))


def dot(a, b, dims):
    return lax.dot_general(a, b, dims, preferred_element_type=F32)


def loop(n, body):
    lax.fori_loop(0, n, lambda i, _: (body(i), 0)[1], 0)


def rows(i):
    return pl.ds(pl.multiple_of(i * 1024, 1024), 1024)


def half(i):
    return pl.ds(pl.multiple_of(i * 512, 512), 512)


def keep_wide(own, k, n, r, c):
    color = k % 2
    for b in range(4):
        bx, by = b // 2, b % 2
        spot = bx * 8 + by * 4 + color * (by * 4 - bx * 4)
        for j in range(2):
            part = r[256 * b : 256 * b + 256, 256 * j : 256 * j + 256].astype(BF).reshape(4, 2, 32, 256)
            for rail in range(2):
                same = 1 - (rail - c) * (rail - c)
                at = same * (k % OWN) + (1 - same) * (OWN + k % OTHER)
                own[at, pl.ds(spot, 4), 2 * n + j] = part[:, rail]


def keep_tall(own, k, b, r, c):
    color, bx, by = k % 2, b // 2, b % 2
    spot = bx * 8 + by * 4 + color * (by * 4 - bx * 4)
    part = r.astype(BF).reshape(4, 2, 4, 32, 256)
    for rail in range(2):
        same = 1 - (rail - c) * (rail - c)
        at = same * (k % OWN) + (1 - same) * (OWN + k % OTHER)
        own[at, pl.ds(spot, 4)] = part[:, rail]


def step_kernel(*refs):
    (x_in, dy_in), stacked = refs[0:2], refs[2:5]
    shards = [w.at[n] for n in range(2) for w in stacked]
    out, total, whole = refs[5], refs[6], refs[7:13]
    acts, silus, slopes, douts, h1, a0 = refs[13:19]
    A, B, D, W, F, S, own, fromtwin, fromfar, fromnear, fromz, squares, box = refs[19:32]
    gsems, glocal, ssems, last, load, tiles = refs[32:38]
    x, y, z, c = place()
    bufs = (own, fromtwin, fromfar, fromnear, fromz, ssems, out, squares)
    copy = pltpu.make_async_copy

    def staged(i, j):
        to = whole[i].at[x, y, z, c]
        if i % 3 == 2:
            return shards[i], W.at[1, pl.ds(128 * (i // 3), 128)], to
        cut = pl.ds(1024 * j, 1024)
        return shards[i].at[:, cut], W.at[0, pl.ds(32 * (16 * (i // 3) + 4 * (i % 3) + j), 32)], to.at[:, cut]

    pieces = [(i, j) for i in range(6) for j in range(1 if i % 3 == 2 else 4)]
    for at, (i, j) in enumerate(pieces):
        copy(*staged(i, j)[:2], glocal.at[at]).start()
    copy(x_in, D.at[0], load.at[0]).start()
    copy(dy_in, B, load.at[1]).start()
    squares[...] = jnp.zeros_like(squares)
    greet()

    def tick(t):
        gather_tick(t, shards, whole, gsems)

    def ticks_at(step, table):
        for at, t in table:
            pl.when(step == at)(lambda t=t: tick(t))

    for at, (i, j) in enumerate(pieces):
        copy(*staged(i, j)[:2], glocal.at[at]).wait()
        copy(*staged(i, j)[1:], glocal.at[at]).start()
    tick(0)
    tick(1)
    for at, (i, j) in enumerate(pieces):
        copy(*staged(i, j)[1:], glocal.at[at]).wait()
    tick(2)
    tick(3)
    copy(x_in, D.at[0], load.at[0]).wait()

    def norm(h):
        wide_h = h.astype(F32)
        return (wide_h * lax.rsqrt(jnp.mean(wide_h * wide_h, -1, keepdims=True) + 1e-6)).astype(BF)

    def first_norm(i):
        at = pl.ds(pl.multiple_of(i * 128, 128), 128)
        A[at] = norm(D[0, at])

    loop(16, first_norm)
    copy(A, a0, load.at[0]).start()
    for t in range(4, 10):
        tick(t)
    copy(A, a0, load.at[0]).wait()

    def wide_quarter(i, q, b):
        return copy(whole[i].at[:, :, :, :, :, rows(q)], W.at[b].reshape(2, 2, 4, 2, 32, 1024), load.at[2 + b])

    def tall_quarter(i, q, b):
        return copy(whole[i].at[q // 2, q % 2], W.at[b].reshape(4, 2, 128, 1024), load.at[2 + b])

    def phase_gu0():
        def gate_up_0(q):
            wide_quarter(0, q, 0).start()
            wide_quarter(1, q, 1).start()
            wide_quarter(0, q, 0).wait()
            wide_quarter(1, q, 1).wait()
            b = q % 2

            @pl.when(q >= 2)
            def _():
                copy(D.at[b], acts.at[0, q - 2], load.at[4 + b]).wait()

            def tile(i):
                ticks_at(4 * q + i, [(2 * j, 10 + j) for j in range(8)])
                m, n, e = i // 2, i % 2, i % 2
                number_of = 4 * q + i

                @pl.when(number_of >= 2)
                def _():
                    copy(F.at[e], silus.at[number_of - 2], tiles.at[0, e]).wait()
                    copy(F.at[2 + e], slopes.at[number_of - 2], tiles.at[1, e]).wait()

                gate = dot(A[rows(m)], W[0, :, half(n)], NN)
                up = dot(A[rows(m)], W[1, :, half(n)], NN)
                s = jax.nn.sigmoid(gate)
                silu = gate * s
                F[e] = silu
                F[2 + e] = up * (s + silu * (1 - s))
                D[b, rows(m), half(n)] = (silu * up).astype(BF)
                copy(F.at[e], silus.at[number_of], tiles.at[0, e]).start()
                copy(F.at[2 + e], slopes.at[number_of], tiles.at[1, e]).start()

            loop(4, tile)
            copy(D.at[b], acts.at[0, q], load.at[4 + b]).start()

        loop(4, gate_up_0)
        for e in range(2):
            copy(F.at[e], silus.at[14 + e], tiles.at[0, e]).wait()
            copy(F.at[2 + e], slopes.at[14 + e], tiles.at[1, e]).wait()
            copy(D.at[e], acts.at[0, 2 + e], load.at[4 + e]).wait()

    phase_gu0()
    tick(18)
    tick(19)

    def act_quarter(n, q, b):
        return copy(acts.at[n, q], D.at[b], load.at[4 + b])

    def phase_down0():
        tall_quarter(2, 0, 0).start()
        act_quarter(0, 0, 0).start()

        def down_0(q):
            b = q % 2
            tall_quarter(2, q, b).wait()
            act_quarter(0, q, b).wait()

            @pl.when(q < 3)
            def _():
                tall_quarter(2, q + 1, 1 - b).start()
                act_quarter(0, q + 1, 1 - b).start()

            def tile(i):
                ticks_at(4 * q + i, [(4 * j, 20 + j) for j in range(4)])
                m, n = i // 2, i % 2
                part = dot(D[b, rows(m)], W[b, :, half(n)], NN)

                @pl.when(q == 0)
                def _():
                    F[i] = part

                @pl.when(q > 0)
                def _():
                    F[i] += part

            loop(4, tile)

        loop(4, down_0)

    phase_down0()
    copy(x_in, D.at[0], load.at[0]).start()
    copy(dy_in, B, load.at[1]).wait()
    copy(x_in, D.at[0], load.at[0]).wait()

    def phase_norm2():
        def second_norm(i):
            at = pl.ds(pl.multiple_of(i * 128, 128), 128)
            m, r = i // 8, pl.ds(pl.multiple_of(i % 8 * 128, 128), 128)
            for n in range(2):
                cut = pl.ds(512 * n, 512)
                D[1, at, cut] = (D[0, at, cut].astype(F32) + F[2 * m + n, r].astype(BF).astype(F32)).astype(BF)
            A[at] = norm(D[1, at])

        loop(16, second_norm)

    phase_norm2()
    copy(D.at[1], h1, load.at[0]).start()

    def phase_hid1():
        tall_quarter(5, 0, 0).start()

        def by_hidden_1(q):
            b = q % 2
            tall_quarter(5, q, b).wait()

            @pl.when(q < 3)
            def _():
                tall_quarter(5, q + 1, 1 - b).start()

            def tile(i):
                ticks_at(4 * q + i, [(8 * j, 24 + j) for j in range(2)])
                m, n, e = i // 2, i % 2, i % 2
                number_of = 4 * q + i

                @pl.when(number_of >= 2)
                def _():
                    copy(S.at[e], douts.at[number_of - 2], tiles.at[0, e]).wait()

                S[e] = dot(B[rows(m)], W[b, half(n)], NT).astype(BF)
                copy(S.at[e], douts.at[number_of], tiles.at[0, e]).start()

            loop(4, tile)

        loop(4, by_hidden_1)
        for e in range(2):
            copy(S.at[e], douts.at[14 + e], tiles.at[0, e]).wait()

    phase_hid1()
    copy(D.at[1], h1, load.at[0]).wait()

    def wide_gradient(k, i):
        def part(n):
            keep_wide(own, k, n, dot(A[...], D[i, :, half(n)], TN), c)

        loop(2, part)
        sum_tick(k, bufs)

    def phase_l1():
        wide_quarter(3, 0, 0).start()
        wide_quarter(4, 0, 1).start()

        def layer_1(q):
            wide_quarter(3, q, 0).wait()
            wide_quarter(4, q, 1).wait()
            copy(douts.at[4 * q], S.at[0], tiles.at[0, 0]).start()

            def tile(i):
                ticks_at(4 * q + i, [(j, 26 + j) for j in range(6)])
                m, n, e = i // 2, i % 2, i % 2
                number_of = 4 * q + i
                copy(douts.at[number_of], S.at[e], tiles.at[0, e]).wait()

                @pl.when(i < 3)
                def _():
                    copy(douts.at[number_of + 1], S.at[1 - e], tiles.at[0, 1 - e]).start()

                @pl.when(number_of >= 2)
                def _():
                    copy(S.at[2 + e], acts.at[1, q, rows(m), half(n)], tiles.at[1, e]).wait()

                def part(j):
                    here = pl.ds(pl.multiple_of(j * 512, 512), 512)
                    there = pl.ds(pl.multiple_of(m * 1024 + j * 512, 512), 512)
                    gate = dot(A[there], W[0, :, half(n)], NN)
                    up = dot(A[there], W[1, :, half(n)], NN)
                    by_act = S[e, here].astype(F32)
                    s = jax.nn.sigmoid(gate)
                    silu = gate * s
                    S[2 + e, here] = (silu * up).astype(BF)
                    D[1, there, half(n)] = (by_act * silu).astype(BF)
                    D[0, there, half(n)] = (by_act * (up * (s + silu * (1 - s)))).astype(BF)

                loop(1024 // 512, part)
                copy(S.at[2 + e], acts.at[1, q, rows(m), half(n)], tiles.at[1, e]).start()

            loop(4, tile)

            def back(i):
                m, n = i // 2, i % 2
                part = dot(D[0, rows(m)], W[0, half(n)], NT) + dot(D[1, rows(m)], W[1, half(n)], NT)

                @pl.when(q == 0)
                def _():
                    F[i] = part

                @pl.when(q > 0)
                def _():
                    F[i] += part

            loop(4, back)

            @pl.when(q < 3)
            def _():
                wide_quarter(3, q + 1, 0).start()
                wide_quarter(4, q + 1, 1).start()

            loop(2, lambda i: wide_gradient(2 * q + i, i))

        loop(4, layer_1)
        for e in range(2):
            copy(S.at[2 + e], acts.at[1, 3, rows(1), half(e)], tiles.at[1, e]).wait()


    phase_l1()
    def tall_gradient(n, k):
        act_quarter(n, 0, 0).start()

        def part(i):
            p, q, b = i // 4, i % 4, i % 2
            act_quarter(n, q, b).wait()

            @pl.when(i < 7)
            def _():
                act_quarter(n, (i + 1) % 4, 1 - b).start()

            r = dot(D[b], B[:, half(p)], TN)
            for j in range(2):
                keep_tall(own, k + 2 * p + j, q, r[:, 256 * j : 256 * j + 256], c)

            @pl.when(q == 3)
            def _():
                loop(2, lambda j: sum_tick(k + 2 * p + j, bufs))

        loop(8, part)

    tall_gradient(1, 8)

    copy(h1, D.at[0], load.at[0]).start()
    copy(a0, A, load.at[1]).start()
    copy(h1, D.at[0], load.at[0]).wait()

    def phase_nback():
        def norm_back(i):
            at = pl.ds(pl.multiple_of(i * 128, 128), 128)
            m, r = i // 8, pl.ds(pl.multiple_of(i % 8 * 128, 128), 128)
            h = D[0, at].astype(F32)
            scale = lax.rsqrt(jnp.mean(h * h, -1, keepdims=True) + 1e-6)
            by_a = [F[2 * m + n, r].astype(BF).astype(F32) for n in range(2)]
            parts = [h[:, 512 * n : 512 * n + 512] for n in range(2)]
            along = sum(jnp.sum(one * part, -1, keepdims=True) for one, part in zip(by_a, parts, strict=True))
            along = along * (scale * scale * scale) * (1 / 1024)
            for n in range(2):
                cut = pl.ds(512 * n, 512)
                by_h = (by_a[n] * scale - parts[n] * along).astype(BF)
                B[at, cut] = (B[at, cut].astype(F32) + by_h.astype(F32)).astype(BF)

        loop(16, norm_back)

    phase_nback()
    tall_gradient(0, 12)

    def kept_tile(number_of, e):
        return (
            copy(silus.at[number_of], F.at[e], tiles.at[0, e]),
            copy(slopes.at[number_of], F.at[2 + e], tiles.at[1, e]),
        )

    copy(a0, A, load.at[1]).wait()
    def phase_l0():
        tall_quarter(2, 0, 0).start()
        for one in kept_tile(0, 0):
            one.start()

        def layer_0(q):
            b = q % 2
            tall_quarter(2, q, b).wait()

            @pl.when(q < 3)
            def _():
                tall_quarter(2, q + 1, 1 - b).start()

            def tile(i):
                m, n, e = i // 2, i % 2, i % 2
                number_of = 4 * q + i
                for one in kept_tile(number_of, e):
                    one.wait()

                @pl.when(number_of < 15)
                def _():
                    for one in kept_tile(number_of + 1, 1 - e):
                        one.start()

                by_act = dot(B[rows(m)], W[b, half(n)], NT).astype(BF).astype(F32)
                D[1, rows(m), half(n)] = (by_act * F[e]).astype(BF)
                D[0, rows(m), half(n)] = (by_act * F[2 + e]).astype(BF)

            loop(4, tile)
            loop(2, lambda i: wide_gradient(16 + 2 * q + i, i))

        loop(4, layer_0)

    phase_l0()
    loop(SUM_AT[-1], lambda t: sum_tick(CHUNKS + t, bufs))
    all_squares(squares, total, box, last)


def stepped(x, dy, weights):
    shards = [jax.ShapeDtypeStruct(w.shape[1:], BF) for n in range(2) for w in weights]
    block, hbm = (4, 32, 256), pl.BlockSpec(memory_space=pl.ANY)
    shape = jax.ShapeDtypeStruct
    results = pl.pallas_call(
        step_kernel,
        name="step",
        out_shape=[shape((CHUNKS,) + block, BF), shape((8, 128), F32)]
        + [shape((2, 2, 4, 2) + s.shape, BF) for s in shards]
        + [
            shape((2, 4, 2048, 1024), BF),
            shape((16, 1024, 512), F32),
            shape((16, 1024, 512), F32),
            shape((16, 1024, 512), BF),
            shape((2048, 1024), BF),
            shape((2048, 1024), BF),
        ],
        in_specs=[hbm] * 5,
        out_specs=[pl.BlockSpec(memory_space=pltpu.VMEM)] * 2 + [hbm] * 12,
        scratch_shapes=[
            pltpu.VMEM((2048, 1024), BF),
            pltpu.VMEM((2048, 1024), BF),
            pltpu.VMEM((2, 2048, 1024), BF),
            pltpu.VMEM((2, 1024, 1024), BF),
            pltpu.VMEM((4, 1024, 512), F32),
            pltpu.VMEM((4, 1024, 512), BF),
            pltpu.VMEM((OWN + OTHER, 16) + block, BF),
            pltpu.VMEM((SLOTS, 16) + block, BF),
            pltpu.VMEM((SLOTS, 8) + block, BF),
            pltpu.VMEM((SLOTS, 4) + block, BF),
            pltpu.VMEM((SLOTS, 3) + block, BF),
            pltpu.VMEM((8, 256), F32),
            pltpu.VMEM((10, 8, 128), F32),
            pltpu.SemaphoreType.DMA((2, CHUNKS, 8)),
            pltpu.SemaphoreType.DMA((18,)),
            pltpu.SemaphoreType.DMA((2, SLOTS, 6)),
            pltpu.SemaphoreType.DMA((2, 6)),
            pltpu.SemaphoreType.DMA((6,)),
            pltpu.SemaphoreType.DMA((2, 2)),
        ],
        compiler_params=pltpu.CompilerParams(collective_id=0, has_side_effects=True, vmem_limit_bytes=67043328),
    )(x, dy, *weights)
    return results[0], results[1]


def solution(mesh):
    def step(x, dy, *arrays):
        weights, m, v = (arrays[i : i + 3] for i in (0, 3, 6))
        sums, squares = stepped(x[0], dy[0], weights)
        layers = [
            [sums[0:8:2], sums[1:8:2], sums[8:12]],
            [sums[16::2], sums[17::2], sums[12:16]],
        ]
        mine = [jnp.stack([layers[1 - n][i].transpose(2, 0, 1, 3).reshape(32, 4096) for n in range(2)]) for i in range(2)]
        mine.append(jnp.stack([layers[1 - n][2].transpose(1, 2, 0, 3).reshape(128, 1024) for n in range(2)]))
        count = 32 * sum(g.size for g in mine)
        factor = jnp.minimum(1.0, 0.5 * lax.rsqrt(squares[0, 0] / count + 1e-30))
        new = [adamw(w.astype(F32), m, v, g.astype(F32) * factor) for w, m, v, g in zip(weights, m, v, mine, strict=True)]
        return tuple(one[which] for which in range(3) for one in new)

    states, cut = P(("rep", "dp"), None, None), P(None, "dp", None)
    return jax.shard_map(
        step,
        mesh=mesh,
        in_specs=(states, states) + (cut,) * 9,
        out_specs=(P("rep", "dp", None),) * 9,
        check_vma=False,
    )
```

time: 977 us -> 618 us (0.63)
  matrix products: 424 us -> 0 us
  Pallas kernels: 470 us -> 586 us
  other arithmetic: 52.7 us -> 8.4 us
    dot_general x15 -> x0, matrix products: 424 us -> none  [the longest x5 154 us: layer(): gate = jnp.dot(a, w['w_gate'], preferred_element_type=jnp.float32)]
    pallas_call x2 -> x1, Pallas kernels: 470 us -> 586 us  [stepped(): pl.pallas_call(step_kernel, name='step', out_shape=[shape((CHUNKS,) + blo...]
    another operation x3 -> x0, other arithmetic: 31.1 us -> none  [step(): jnp.stack([grads[n][name].reshape(2, 2, 4, 2, -1, grads[n][name].shape[-1...]
    unnamed x32 -> x8, local copies, waits for them, and re-layouts: 13.3 us -> 0.03 us
    transpose x0 -> x7, local copies, waits for them, and re-layouts: none -> 10.6 us  [the longest x4 5.53 us: step(): layers[1 - n][i].transpose(2, 0, 1, 3).reshape(32, 4096)]
where the time goes in v2:
time: 618 us; the launch traced here: 617 us
  Pallas kernels  586 us (95%)
  local copies, waits for them, and re-layouts  20.8 us (3%)
  other arithmetic  8.4 us (1%)
    pallas_call x1, Pallas kernels, stepped(): pl.pallas_call(step_kernel, name='step', out_shape=[shape((CHUNKS,) + blo...  586 us

profile of v2, /device:TPU:0, one launch (start us, length us, event | category | flops | bytes accessed | tf_op | source)
XLA Modules:
  0.0 616.6 jit_solution(6569313366139402995)
XLA Ops:
  0.6 586.0 %step.1 = (bf16[24,4,32,256]{3,2,1,0:T(8,128)(2,1)}, f32[8,128]{1,0:T(8,128)}, bf16[2,2,4,2,32,4096]{5,4,3,2,1,0:T(8,128)(2,1)}, bf16[2,2,4,2,32,4096]{5,4,3,2,1...) custom-call(bf16[2048,1024]{1,0:T(8,128)(2,1)} %bitcast.15, ...), custom_call_target="tpu_custom_call" | custom-call | tf_op jit(solution)/shard_map/step/pallas_call | solution.py:617
  586.7 0.0 copy-start
  586.7 0.0 copy-start.1
  586.7 0.0 copy-start.2
  586.7 0.0 copy-start.3
  586.7 1.3 slice.23
  588.8 2.3 slice_bitcast_fusion.1
  591.1 0.9 copy.24
  592.0 1.1 stack_reshape.22
  593.1 1.9 copy.25
  594.9 1.8 stack_reshape.23
  596.8 0.9 copy.23
  597.7 1.1 stack_reshape.21
  598.8 0.9 copy.22
  599.7 1.1 stack_reshape.20
  600.8 1.9 copy.21
  602.7 1.8 stack_reshape.19
  604.5 1.9 copy.20
  606.4 1.8 stack_reshape.18
  608.2 0.0 copy-done
  608.2 3.4 fusion.8
  611.6 0.0 copy-done.1
  611.7 0.0 copy-done.2
  611.7 0.0 copy-done.3
  611.7 5.0 fusion.2
Async XLA Ops:
  586.7 21.5 %copy-start = (bf16[2,128,1024]{2,1,0:T(8,128)(2,1)S(1)}, bf16[2,128,1024]{2,1,0:T(8,128)(2,1)}, u32[]{:S(2)}) copy-start(bf16[2,128,1024]{2,1,0:T(8,128)(2,1)} %refs_4_.1) | copy-start | bytes 1572868
  586.7 24.9 %copy-start.1 = (bf16[2,32,4096]{2,1,0:T(8,128)(2,1)S(1)}, bf16[2,32,4096]{2,1,0:T(8,128)(2,1)}, u32[]{:S(2)}) copy-start(bf16[2,32,4096]{2,1,0:T(8,128)(2,1)} %refs_2_.1) | copy-start | bytes 1572868
  586.7 24.9 %copy-start.2 = (bf16[2,32,4096]{2,1,0:T(8,128)(2,1)S(1)}, bf16[2,32,4096]{2,1,0:T(8,128)(2,1)}, u32[]{:S(2)}) copy-start(bf16[2,32,4096]{2,1,0:T(8,128)(2,1)} %refs_3_.1) | copy-start | bytes 1572868
  586.7 24.9 %copy-start.3 = (f32[2,32,4096]{2,1,0:T(8,128)S(1)}, f32[2,32,4096]{2,1,0:T(8,128)}, u32[]{:S(2)}) copy-start(f32[2,32,4096]{2,1,0:T(8,128)} %param.19) | copy-start | bytes 3145732

commit v3 on v2

v3 whole, which is shorter than its diff:
```python
import jax
import jax.numpy as jnp
from jax import lax
from jax.experimental import pallas as pl
from jax.experimental.pallas import tpu as pltpu
from jax.sharding import PartitionSpec as P

BF, F32 = jnp.bfloat16, jnp.float32
MESH = pl.DeviceIdType.MESH
CHUNKS = 48
SLOTS, OWN, OTHER = 12, 15, 8


def adamw(w, m, v, g):
    m = 0.9 * m + 0.1 * g
    v = 0.95 * v + 0.05 * g * g
    step = m * lax.rsqrt(v + 1e-8) + 0.1 * w
    return (w - 0.02 * step).astype(jnp.bfloat16), m, v


HERE = []


def find():
    me = lax.axis_index("dp")
    HERE[:] = [lax.div(me, 16), lax.rem(lax.div(me, 8), 2), lax.rem(lax.div(me, 2), 4), lax.rem(me, 2)]


def place():
    return tuple(HERE)


def mod(a, b):
    return a % b if isinstance(a, int) else lax.rem(a, b)


def div(a, b):
    return a // b if isinstance(a, int) else lax.div(a, b)


def number(x, y, z, c):
    return ((x * 2 + y) * 4 + z) * 2 + c


def greet():
    x, y, z, c = place()
    barrier = pltpu.get_barrier_semaphore()
    others = [(1 - x, y, z, c), (x, 1 - y, z, c), (x, y, z, 1 - c)]
    others += [(x, y, (z + hop) % 4, c) for hop in (1, 2, 3)]
    for other in others:
        pl.semaphore_signal(barrier, 1, device_id={"dp": number(*other)}, device_id_type=MESH)
    pl.semaphore_wait(barrier, len(others))


def send(src, dst, sems, where):
    return pltpu.make_async_remote_copy(
        src_ref=src, dst_ref=dst, send_sem=sems[0], recv_sem=sems[1], device_id={"dp": number(*where)}, device_id_type=MESH
    )


GATHER_AT = (0, 3, 5, 8, 10)
DONE = GATHER_AT[-1]


def route(k):
    x, y, z, c = place()
    color = mod(k, 2)
    f, n = x + color * (y - x), y + color * (x - y)
    far = (x + (1 - color) * (1 - 2 * x), y + color * (1 - 2 * y), z, c)
    near = (x + color * (1 - 2 * x), y + (1 - color) * (1 - 2 * y), z, c)
    ups = [(x, y, (z + hop) & 3, c) for hop in (1, 2, 3)]
    return f, n, z, c, far, near, ups, (x, y, z, 1 - c)


def landed(pieces, pack, sem):
    part = pack.at[pl.ds(0, pieces)]
    pltpu.make_async_copy(part, part, sem).wait()


def gather_copies(k, stage, pack, whole, sent, came):
    f, n, z, c, far, near, ups, twin = route(k)
    every, z_first = slice(None), k % 3 < 2

    def go(i, where, *at):
        part = whole.at[(k,) + at]
        return send(part, part, (sent.at[0], came.at[k, i]), where)

    def own(i, where):
        return send(pack.at[k], whole.at[k, f, n, z, c], (sent.at[1], came.at[k, i]), where)

    if stage == 0:
        return [own(0, up) for up in ups] if z_first else [own(1, near)]
    if stage == 1:
        return [go(1, near, f, n, every, c)] if z_first else [go(0, up, f, every, z, c) for up in ups]
    if stage == 2:
        return [go(2, far, f, every, every, c)]
    return [go(3, twin, every, every, every, c)]


def gather_tick(t, bufs):
    pack, came = bufs[0], bufs[3]
    for stage in (4, 3, 2, 1, 0):
        k = t - GATHER_AT[stage]
        if not 0 <= k < CHUNKS:
            continue
        z_first = k % 3 < 2
        if stage == 1:
            landed(3 if z_first else 1, pack, came.at[k, 0 if z_first else 1])
        if stage == 2:
            landed(4 if z_first else 6, pack, came.at[k, 1 if z_first else 0])
        if stage == 3:
            landed(8, pack, came.at[k, 2])
        if stage == 4:
            landed(16, pack, came.at[k, 3])
        else:
            for copy in gather_copies(k, stage, *bufs):
                copy.start()


SUM_AT = (0, 1, 3, 6, 8)


def wide(ref, *at):
    return ref[at].astype(F32)


def sum_stages(k, own, fromtwin, fromfar, fromnear, fromz, sems, out, squares, put):
    f, n, z, c, far, near, ups, twin = route(k)
    slot, mine = mod(k, SLOTS), mod(k, OWN)
    every = slice(None)

    def pair(i):
        return sems.at[slot, 5], sems.at[slot, 1 + i]

    def two(*at):
        return wide(own, mine, *at) + wide(fromtwin, slot, *at)

    def to_twin():
        return send(own.at[OWN + mod(k, OTHER)], fromtwin.at[slot], (sems.at[slot, 0], sems.at[slot, 1]), twin)

    def to_far():
        return send(fromtwin.at[slot, 1 - f], fromfar.at[slot], pair(1), far)

    def first():
        to_twin().start()

    def second():
        to_twin().wait()

        def add(i, _):
            at = (1 - f, i // 2, pl.ds(2 * (i % 2), 2))
            fromtwin[(slot,) + at] = two(*at).astype(BF)
            return 0

        lax.fori_loop(0, 4, add, 0)
        to_far().start()

    def near_first():
        return send(fromtwin.at[slot, f, 1 - n], fromnear.at[slot], pair(2), near)

    def z_last(hop):
        to = ups[hop][2]
        return send(fromtwin.at[slot, f, n, to], fromz.at[slot, hop, 0], pair(3), ups[hop])

    def third_near():
        to_far().wait_recv()

        def add(i, _):
            at = (1 - n, pl.ds(2 * i, 2))
            fromtwin[(slot, f) + at] = (two(f, *at) + wide(fromfar, slot, *at)).astype(BF)
            return 0

        lax.fori_loop(0, 2, add, 0)
        near_first().start()

    def fourth_near():
        near_first().wait_recv()
        for hop in range(3):
            to = ups[hop][2]
            total = two(f, n, to) + wide(fromfar, slot, n, to) + wide(fromnear, slot, to)
            fromtwin[slot, f, n, to] = total.astype(BF)
            z_last(hop).start()

    def fifth_near():
        landed(3, out, sems.at[slot, 4])
        return wide(fromnear, slot, z) + wide(fromz, slot, 0, 0) + wide(fromz, slot, 1, 0) + wide(fromz, slot, 2, 0)

    def z_first(hop):
        to = ups[hop][2]
        return send(fromtwin.at[slot, f, every, to], fromz.at[slot, hop], pair(3), ups[hop])

    def near_last():
        return send(fromtwin.at[slot, f, 1 - n, z], fromnear.at[slot, 0], pair(2), near)

    def third_z():
        to_far().wait_recv()
        for hop in range(3):
            to = ups[hop][2]
            for i in range(2):
                fromtwin[slot, f, i, to] = (two(f, i, to) + wide(fromfar, slot, i, to)).astype(BF)
            z_first(hop).start()

    def along_z(i):
        return wide(fromz, slot, 0, i) + wide(fromz, slot, 1, i) + wide(fromz, slot, 2, i)

    def fourth_z():
        landed(6, out, sems.at[slot, 4])
        total = two(f, 1 - n, z) + wide(fromfar, slot, 1 - n, z) + along_z(1 - n)
        fromtwin[slot, f, 1 - n, z] = total.astype(BF)
        near_last().start()

    def fifth_z():
        near_last().wait_recv()
        return along_z(n) + wide(fromnear, slot, 0)

    def fifth(rest):
        landed(15, out, sems.at[slot, 5])
        total = (two(f, n, z) + wide(fromfar, slot, n, z) + rest()).astype(BF)
        out[k] = total
        put(k)
        square = total.astype(F32)
        square = square * square
        squares[...] += jnp.sum(square.reshape(16, 8, 128), axis=0)

    def last_near():
        fifth(fifth_near)

    def last_z():
        fifth(fifth_z)

    return (first, second, (third_near, third_z), (fourth_near, fourth_z), (last_near, last_z))


def sum_tick(t, bufs):
    for stage in (4, 3, 2, 1, 0):
        k = t - SUM_AT[stage]

        @pl.when(jnp.logical_and(k >= 0, k < CHUNKS))
        def _():
            if stage < 2:
                sum_stages(k, *bufs)[stage]()
            else:
                pl.when(mod(k, 3) < 2)(lambda: sum_stages(k, *bufs)[stage][0]())
                pl.when(mod(k, 3) >= 2)(lambda: sum_stages(k, *bufs)[stage][1]())


def all_squares(squares, total, box, sems):
    x, y, z, c = place()
    box[0] = jnp.broadcast_to(jnp.sum(squares[...]), (8, 128))
    for i, other in enumerate([(x, y, z, 1 - c), (1 - x, y, z, c), (x, 1 - y, z, c)]):
        copy = send(box.at[i], box.at[7 + i], (sems.at[0, i], sems.at[1, i]), other)
        copy.start()
        copy.wait()
        box[i + 1] = box[i] + box[7 + i]
    copies = [
        send(box.at[3], box.at[3 + hop], (sems.at[0, 2 + hop], sems.at[1, 2 + hop]), (x, y, (z + hop) % 4, c)) for hop in (1, 2, 3)
    ]
    for copy in copies:
        copy.start()
    for copy in copies:
        copy.wait()
    total[...] = (box[3] + box[5]) + (box[4] + box[6])


NN, NT, TN = (((1,), (0,)), ((), ())), (((1,), (1,)), ((), ())), (((0,), (0,)), ((), ()))


def dot(a, b, dims):
    return lax.dot_general(a, b, dims, preferred_element_type=F32)


def loop(n, body):
    lax.fori_loop(0, n, lambda i, _: (body(i), 0)[1], 0)


def rows(i):
    return pl.ds(pl.multiple_of(i * 1024, 1024), 1024)


def half(i):
    return pl.ds(pl.multiple_of(i * 512, 512), 512)


def spots(k, rail, c, b):
    same = 1 - (rail - c) * (rail - c)
    at = same * mod(k, OWN) + (1 - same) * (OWN + mod(k, OTHER))
    color, bx, by = mod(k, 2), div(b, 2), mod(b, 2)
    return at, bx + color * (by - bx), by + color * (bx - by)


def keep_wide(own, k, r, c):
    for b in range(4):
        for j in range(4):
            part = r[256 * b : 256 * b + 256, 128 * j : 128 * j + 128].astype(BF).reshape(4, 2, 32, 128)
            for rail in range(2):
                at, far, near = spots(k, rail, c, b)
                own[at, far, near, :, j] = part[:, rail]


def keep_tall(own, k, b, r, c):
    part = r.astype(BF).reshape(4, 2, 4, 32, 128)
    for rail in range(2):
        at, far, near = spots(k, rail, c, b)
        own[at, far, near] = part[:, rail]


def step_kernel(*refs):
    (x_in, dy_in), shards = refs[0:2], refs[2:5]
    total, grads, whole = refs[5], refs[6:9], refs[9]
    acts, silus, slopes, douts, hidden, h1, a0 = refs[10:17]
    A, B, D, W, F, S, pack, own, fromtwin, fromfar, fromnear, fromz, squares, box = refs[17:31]
    gsems, glocal, ssems, last, load, tiles = refs[31:37]
    find()
    x, y, z, c = place()
    copy = pltpu.make_async_copy

    def packed(k):
        if 16 <= k < 32:
            return [copy(shards[2].at[k // 24].reshape(4, 32, 1024).at[:, :, pl.ds(k % 8 * 128, 128)], pack.at[k], glocal.at[0])]
        first = (k % 32) // 4 * 1024 + (k % 4) // 2 * 512
        return [copy(shards[k % 2].at[k // 32, :, pl.ds(first + 128 * j, 128)], pack.at[k, j], glocal.at[0]) for j in range(4)]

    for k in range(CHUNKS):
        for one in packed(k):
            one.start()
    copy(x_in, D.at[0], load.at[0]).start()
    copy(dy_in, B, load.at[1]).start()
    squares[...] = jnp.zeros_like(squares)
    greet()
    copy(pack, pack, glocal.at[0]).wait()

    def sent_all(i):
        first = sum(3 if k % 3 < 2 else 1 for k in range(CHUNKS))
        part = whole.reshape(32 * CHUNKS, 4, 32, 128).at[pl.ds(0, first if i else 31 * CHUNKS - first)]
        copy(part, part, glocal.at[2 + i]).wait()

    def put(k):
        n, first = 1 - div(k, 24), div(mod(k, 32), 4) * 1024 + mod(k, 2) * 512
        flat = jnp.logical_or(k < 16, k >= 32)
        for i in range(2):

            @pl.when(jnp.logical_and(flat, div(mod(k, 4), 2) == i))
            def _():
                for j in range(4):
                    cut = pl.ds(pl.multiple_of(first + 128 * j, 128), 128)
                    copy(pack.at[k, j], grads[i].at[n, :, cut], glocal.at[0]).start()

        @pl.when(jnp.logical_not(flat))
        def _():
            cut = pl.ds(pl.multiple_of(mod(k, 8) * 128, 128), 128)
            copy(pack.at[k], grads[2].at[n].reshape(4, 32, 1024).at[:, :, cut], glocal.at[0]).start()

    bufs = (own, fromtwin, fromfar, fromnear, fromz, ssems, pack, squares, put)

    def tick(t):
        gather_tick(t, (pack, whole, glocal.at[pl.ds(2, 2)], gsems))

    def ticks_at(step, first, count, every=1):
        for i in range(count):
            pl.when(step == i * every)(lambda i=i: tick(first + i))

    def sum_at(when, t):
        pl.when(when)(lambda: sum_tick(t, bufs))

    tick(0)
    tick(1)
    for k in range(CHUNKS):
        f, n = route(k)[:2]
        copy(pack.at[k], whole.at[k, f, n, z, c], glocal.at[1]).start()
    copy(pack, pack, glocal.at[1]).wait()
    tick(2)
    tick(3)
    copy(x_in, D.at[0], load.at[0]).wait()

    def norm(h):
        wide_h = h.astype(F32)
        return (wide_h * lax.rsqrt(jnp.mean(wide_h * wide_h, -1, keepdims=True) + 1e-6)).astype(BF)

    def first_norm(i):
        at = pl.ds(pl.multiple_of(i * 128, 128), 128)
        A[at] = norm(D[0, at])

    loop(16, first_norm)
    copy(A, a0, load.at[0]).start()
    for t in range(DONE):
        tick(4 + t)
    copy(A, a0, load.at[0]).wait()

    def wide_quarter(n, i, q, b):
        def part(at):
            blk, k = at // 2, 32 * n + 4 * q + 2 * (at % 2) + i
            bx, by = blk // 2, blk % 2
            for j in range(4):
                cut = pl.ds(pl.multiple_of(at % 2 * 512 + 128 * j, 128), 128)
                src = whole.at[k, bx + i * (by - bx), by + i * (bx - by), :, :, j]
                copy(src, W.at[b].reshape(4, 4, 2, 32, 1024).at[blk, :, :, :, cut], load.at[2 + b]).start()

        loop(8, part)

    def tall_quarter(n, q, b):
        def part(j):
            color, bx, by = j % 2, q // 2, q % 2
            cut = pl.ds(pl.multiple_of(128 * j, 128), 128)
            src = whole.at[16 + 8 * n + j, bx + color * (by - bx), by + color * (bx - by)]
            copy(src, W.at[b].reshape(4, 2, 4, 32, 1024).at[:, :, :, :, cut], load.at[2 + b]).start()

        loop(8, part)

    def loaded(b):
        copy(W.at[b], W.at[b], load.at[2 + b]).wait()

    def phase_gu0():
        def gate_up_0(q):
            wide_quarter(0, 0, q, 0)
            wide_quarter(0, 1, q, 1)
            loaded(0)
            loaded(1)
            b = q % 2

            @pl.when(q >= 2)
            def _():
                copy(D.at[b], acts.at[0, q - 2], load.at[4 + b]).wait()

            def tile(i):
                ticks_at(4 * q + i, DONE + 4, 16)
                m, n, e = i // 2, i % 2, i % 2
                number_of = 4 * q + i

                @pl.when(number_of >= 2)
                def _():
                    copy(F.at[e], silus.at[number_of - 2], tiles.at[0, e]).wait()
                    copy(F.at[2 + e], slopes.at[number_of - 2], tiles.at[1, e]).wait()

                def part(j):
                    here = half(j)
                    there = pl.ds(pl.multiple_of(m * 1024 + j * 512, 512), 512)
                    gate = dot(A[there], W[0, :, half(n)], NN)
                    up = dot(A[there], W[1, :, half(n)], NN)
                    s = jax.nn.sigmoid(gate)
                    silu = gate * s
                    F[e, here] = silu
                    F[2 + e, here] = up * (s + silu * (1 - s))
                    D[b, there, half(n)] = (silu * up).astype(BF)

                loop(2, part)
                copy(F.at[e], silus.at[number_of], tiles.at[0, e]).start()
                copy(F.at[2 + e], slopes.at[number_of], tiles.at[1, e]).start()

            loop(4, tile)
            copy(D.at[b], acts.at[0, q], load.at[4 + b]).start()

        loop(4, gate_up_0)
        for e in range(2):
            copy(F.at[e], silus.at[14 + e], tiles.at[0, e]).wait()
            copy(F.at[2 + e], slopes.at[14 + e], tiles.at[1, e]).wait()
            copy(D.at[e], acts.at[0, 2 + e], load.at[4 + e]).wait()

    phase_gu0()
    for t in range(4):
        tick(DONE + 20 + t)

    def act_quarter(n, q, b):
        return copy(acts.at[n, q], D.at[b], load.at[4 + b])

    def phase_down0():
        tall_quarter(0, 0, 0)
        act_quarter(0, 0, 0).start()

        def down_0(q):
            b = q % 2
            loaded(b)
            act_quarter(0, q, b).wait()

            @pl.when(q < 3)
            def _():
                tall_quarter(0, q + 1, 1 - b)
                act_quarter(0, q + 1, 1 - b).start()

            def tile(i):
                ticks_at(4 * q + i, DONE + 24, 8, 2)
                m, n = i // 2, i % 2
                part = dot(D[b, rows(m)], W[b, :, half(n)], NN)

                @pl.when(q == 0)
                def _():
                    F[i] = part

                @pl.when(q > 0)
                def _():
                    F[i] += part

            loop(4, tile)

        loop(4, down_0)

    phase_down0()
    copy(x_in, D.at[0], load.at[0]).start()
    copy(dy_in, B, load.at[1]).wait()
    copy(x_in, D.at[0], load.at[0]).wait()

    def phase_norm2():
        def second_norm(i):
            at = pl.ds(pl.multiple_of(i * 128, 128), 128)
            m, r = i // 8, pl.ds(pl.multiple_of(i % 8 * 128, 128), 128)
            for n in range(2):
                cut = pl.ds(512 * n, 512)
                D[1, at, cut] = (D[0, at, cut].astype(F32) + F[2 * m + n, r].astype(BF).astype(F32)).astype(BF)
            A[at] = norm(D[1, at])

        loop(16, second_norm)

    phase_norm2()
    copy(D.at[1], h1, load.at[0]).start()

    def phase_hid1():
        tall_quarter(1, 0, 0)

        def by_hidden_1(q):
            b = q % 2
            loaded(b)

            @pl.when(q < 3)
            def _():
                tall_quarter(1, q + 1, 1 - b)

            def tile(i):
                ticks_at(4 * q + i, DONE + 32, 4, 4)
                m, n, e = i // 2, i % 2, i % 2
                number_of = 4 * q + i

                @pl.when(number_of >= 2)
                def _():
                    copy(S.at[e], douts.at[number_of - 2], tiles.at[0, e]).wait()

                S[e] = dot(B[rows(m)], W[b, half(n)], NT).astype(BF)
                copy(S.at[e], douts.at[number_of], tiles.at[0, e]).start()

            loop(4, tile)

        loop(4, by_hidden_1)
        for e in range(2):
            copy(S.at[e], douts.at[14 + e], tiles.at[0, e]).wait()

    phase_hid1()
    copy(D.at[1], h1, load.at[0]).wait()

    def wide_gradient(k, i):
        keep_wide(own, k + i, dot(A[...], D[i // 2, :, half(i % 2)], TN), c)

    def phase_l1():
        wide_quarter(1, 0, 0, 0)
        wide_quarter(1, 1, 0, 1)

        def layer_1(q):
            loaded(0)
            loaded(1)
            pl.when(q == 1)(lambda: sent_all(1))
            copy(douts.at[4 * q], S.at[0], tiles.at[0, 0]).start()

            def tile(i):
                for j in range(6):
                    pl.when(4 * q + i == 4 * (j // 2) + 2 * (j % 2) + 1)(lambda j=j: tick(DONE + 36 + 4 * (j // 2) + j % 2))
                sum_at(i % 2 == 1, 4 * q + i // 2 - 3)
                m, n, e = i // 2, i % 2, i % 2
                number_of = 4 * q + i
                copy(douts.at[number_of], S.at[e], tiles.at[0, e]).wait()

                @pl.when(i < 3)
                def _():
                    copy(douts.at[number_of + 1], S.at[1 - e], tiles.at[0, 1 - e]).start()

                @pl.when(number_of >= 2)
                def _():
                    copy(S.at[2 + e], acts.at[1, q, rows(m), half(n)], tiles.at[1, e]).wait()

                def part(j):
                    here = pl.ds(pl.multiple_of(j * 512, 512), 512)
                    there = pl.ds(pl.multiple_of(m * 1024 + j * 512, 512), 512)
                    gate = dot(A[there], W[0, :, half(n)], NN)
                    up = dot(A[there], W[1, :, half(n)], NN)
                    by_act = S[e, here].astype(F32)
                    s = jax.nn.sigmoid(gate)
                    silu = gate * s
                    S[2 + e, here] = (silu * up).astype(BF)
                    D[1, there, half(n)] = (by_act * silu).astype(BF)
                    D[0, there, half(n)] = (by_act * (up * (s + silu * (1 - s)))).astype(BF)

                loop(1024 // 512, part)
                copy(S.at[2 + e], acts.at[1, q, rows(m), half(n)], tiles.at[1, e]).start()

            loop(4, tile)

            for i in range(2):
                copy(D.at[i], hidden.at[2 * q + i], load.at[4 + i]).start()

            def part(i):
                for j in range(6):
                    pl.when(4 * q + i == 4 * (j // 2) + 2 * (j % 2))(lambda j=j: tick(DONE + 38 + 4 * (j // 2) + j % 2))

                @pl.when(jnp.logical_and(q < 3, i == 3))
                def _():
                    wide_quarter(1, 0, q + 1, 0)
                    wide_quarter(1, 1, q + 1, 1)

                wide_gradient(4 * q, i)
                sum_at(i % 2 == 1, 4 * q + i // 2 - 1)

            loop(4, part)
            for i in range(2):
                copy(D.at[i], hidden.at[2 * q + i], load.at[4 + i]).wait()

        loop(4, layer_1)
        for e in range(2):
            copy(S.at[2 + e], acts.at[1, 3, rows(1), half(e)], tiles.at[1, e]).wait()


    phase_l1()
    sent_all(0)
    def tall_part(b, k, i):
        p, q = i // 4, i % 4
        r = dot(D[b], B[:, half(p)], TN)
        for j in range(4):
            keep_tall(own, k + 4 * p + j, q, r[:, 128 * j : 128 * j + 128], c)

    def back_part(i):
        return copy(hidden.at[i], D.at[0], load.at[4])

    def phase_back():
        def start(i):
            back_part(i).start()

            @pl.when(i % 2 == 0)
            def _():
                wide_quarter(1, 0, i // 2, 0)

            @pl.when(i % 2 == 1)
            def _():
                wide_quarter(1, 1, i // 2, 1)

        start(0)
        act_quarter(1, 0, 1).start()

        def back(i):
            back_part(i).wait()
            loaded(i % 2)

            def tile(j):
                m, n = j // 2, j % 2
                part = dot(D[0, rows(m)], W[i % 2, half(n)], NT)

                @pl.when(i == 0)
                def _():
                    F[j] = part

                @pl.when(i > 0)
                def _():
                    F[j] += part

            loop(4, tile)
            pl.when(i < 7)(lambda: start(i + 1))
            act_quarter(1, i % 4, 1).wait()
            tall_part(1, 16, i)
            pl.when(i < 7)(lambda: act_quarter(1, (i + 1) % 4, 1).start())
            sum_tick(13 + i, bufs)

        loop(8, back)

    phase_back()

    copy(h1, D.at[0], load.at[0]).start()
    copy(a0, A, load.at[1]).start()
    copy(h1, D.at[0], load.at[0]).wait()

    def phase_nback():
        def norm_back(i):
            at = pl.ds(pl.multiple_of(i * 128, 128), 128)
            m, r = i // 8, pl.ds(pl.multiple_of(i % 8 * 128, 128), 128)
            h = D[0, at].astype(F32)
            scale = lax.rsqrt(jnp.mean(h * h, -1, keepdims=True) + 1e-6)
            by_a = [F[2 * m + n, r].astype(BF).astype(F32) for n in range(2)]
            parts = [h[:, 512 * n : 512 * n + 512] for n in range(2)]
            along = sum(jnp.sum(one * part, -1, keepdims=True) for one, part in zip(by_a, parts, strict=True))
            along = along * (scale * scale * scale) * (1 / 1024)
            for n in range(2):
                cut = pl.ds(512 * n, 512)
                by_h = (by_a[n] * scale - parts[n] * along).astype(BF)
                B[at, cut] = (B[at, cut].astype(F32) + by_h.astype(F32)).astype(BF)

        loop(16, norm_back)

    sum_tick(21, bufs)
    phase_nback()
    sum_tick(22, bufs)
    def phase_tall0():
        act_quarter(0, 0, 0).start()

        def part(i):
            b = i % 2
            act_quarter(0, i % 4, b).wait()
            pl.when(i < 7)(lambda: act_quarter(0, (i + 1) % 4, 1 - b).start())
            tall_part(b, 24, i)
            sum_at(i % 2 == 1, 23 + i // 2)

        loop(8, part)

    phase_tall0()

    def kept_tile(number_of, e):
        return (
            copy(silus.at[number_of], F.at[e], tiles.at[0, e]),
            copy(slopes.at[number_of], F.at[2 + e], tiles.at[1, e]),
        )

    copy(a0, A, load.at[1]).wait()
    def phase_l0():
        tall_quarter(0, 0, 0)
        for one in kept_tile(0, 0):
            one.start()

        def layer_0(q):
            b = q % 2
            loaded(b)

            @pl.when(q < 3)
            def _():
                tall_quarter(0, q + 1, 1 - b)

            def tile(i):
                sum_at(i % 2 == 1, 27 + 5 * q + i // 2)
                m, n, e = i // 2, i % 2, i % 2
                number_of = 4 * q + i
                for one in kept_tile(number_of, e):
                    one.wait()

                @pl.when(number_of < 15)
                def _():
                    for one in kept_tile(number_of + 1, 1 - e):
                        one.start()

                by_act = dot(B[rows(m)], W[b, half(n)], NT).astype(BF).astype(F32)
                D[1, rows(m), half(n)] = (by_act * F[e]).astype(BF)
                D[0, rows(m), half(n)] = (by_act * F[2 + e]).astype(BF)

            loop(4, tile)
            def part(i):
                wide_gradient(32 + 4 * q, i)
                sum_at(i != 1, 29 + 5 * q + (i + 1) // 2)

            loop(4, part)

        loop(4, layer_0)

    phase_l0()
    loop(SUM_AT[-1] + 1, lambda t: sum_tick(CHUNKS - 1 + t, bufs))
    all_squares(squares, total, box, last)
    copy(pack, pack, glocal.at[0]).wait()


def stepped(x, dy, weights):
    block, hbm, shape = (4, 32, 128), pl.BlockSpec(memory_space=pl.ANY), jax.ShapeDtypeStruct
    results = pl.pallas_call(
        step_kernel,
        name="step",
        out_shape=[shape((8, 128), F32)]
        + [shape(w.shape, BF) for w in weights]
        + [
            shape((CHUNKS, 2, 2, 4, 2) + block, BF),
            shape((2, 4, 2048, 1024), BF),
            shape((16, 1024, 512), F32),
            shape((16, 1024, 512), F32),
            shape((16, 1024, 512), BF),
            shape((8, 2048, 1024), BF),
            shape((2048, 1024), BF),
            shape((2048, 1024), BF),
        ],
        in_specs=[hbm] * 5,
        out_specs=[pl.BlockSpec(memory_space=pltpu.VMEM)] + [hbm] * 11,
        scratch_shapes=[
            pltpu.VMEM((2048, 1024), BF),
            pltpu.VMEM((2048, 1024), BF),
            pltpu.VMEM((2, 2048, 1024), BF),
            pltpu.VMEM((2, 1024, 1024), BF),
            pltpu.VMEM((4, 1024, 512), F32),
            pltpu.VMEM((4, 1024, 512), BF),
            pltpu.VMEM((CHUNKS,) + block, BF),
            pltpu.VMEM((OWN + OTHER, 2, 2, 4) + block, BF),
            pltpu.VMEM((SLOTS, 2, 2, 4) + block, BF),
            pltpu.VMEM((SLOTS, 2, 4) + block, BF),
            pltpu.VMEM((SLOTS, 4) + block, BF),
            pltpu.VMEM((SLOTS, 3, 2) + block, BF),
            pltpu.VMEM((8, 128), F32),
            pltpu.VMEM((10, 8, 128), F32),
            pltpu.SemaphoreType.DMA((CHUNKS, 4)),
            pltpu.SemaphoreType.DMA((4,)),
            pltpu.SemaphoreType.DMA((SLOTS, 6)),
            pltpu.SemaphoreType.DMA((2, 6)),
            pltpu.SemaphoreType.DMA((6,)),
            pltpu.SemaphoreType.DMA((2, 2)),
        ],
        compiler_params=pltpu.CompilerParams(collective_id=0, has_side_effects=True, vmem_limit_bytes=67043328),
    )(x, dy, *weights)
    return results[0], results[1:4]


def solution(mesh):
    def step(x, dy, *arrays):
        weights, m, v = (arrays[i : i + 3] for i in (0, 3, 6))
        squares, mine = stepped(x[0], dy[0], weights)
        count = 32 * sum(g.size for g in mine)
        factor = jnp.minimum(1.0, 0.5 * lax.rsqrt(squares[0, 0] / count + 1e-30))
        new = [adamw(w.astype(F32), m, v, g.astype(F32) * factor) for w, m, v, g in zip(weights, m, v, mine, strict=True)]
        return tuple(one[which] for which in range(3) for one in new)

    states, cut = P(("rep", "dp"), None, None), P(None, "dp", None)
    return jax.shard_map(
        step,
        mesh=mesh,
        in_specs=(states, states) + (cut,) * 9,
        out_specs=(P("rep", "dp", None),) * 9,
        check_vma=False,
    )
```

time: 618 us -> 561 us (0.908)
  Pallas kernels: 586 us -> 548 us
  local copies, waits for them, and re-layouts: 20.8 us -> 1.19 us
    pallas_call x1, Pallas kernels: 586 us -> 548 us  [stepped(): pl.pallas_call(step_kernel, name='step', out_shape=[shape((8, 128), F32)]...]
    transpose x7 -> x0, local copies, waits for them, and re-layouts: 10.6 us -> none  [the longest x4 5.53 us: step(): layers[1 - n][i].transpose(2, 0, 1, 3).reshape(32, 4096)]
    another operation x6 -> x0, local copies, waits for them, and re-layouts: 8.84 us -> none  [the longest x4 5.91 us: step(): jnp.stack([layers[1 - n][i].transpose(2, 0, 1, 3).reshape(32, 4096) for n...]
where the time goes in v3:
time: 561 us; the launch traced here: 560 us
  Pallas kernels  548 us (98%)
  other arithmetic  9.37 us (2%)
    pallas_call x1, Pallas kernels, stepped(): pl.pallas_call(step_kernel, name='step', out_shape=[shape((8, 128), F32)]...  548 us

profile of v3, /device:TPU:0, one launch (start us, length us, event | category | flops | bytes accessed | tf_op | source)
XLA Modules:
  0.0 559.6 jit_solution(5700818874199177720)
XLA Ops:
  0.6 547.7 %step.1 = (f32[8,128]{1,0:T(8,128)}, bf16[2,32,4096]{2,1,0:T(8,128)(2,1)}, bf16[2,32,4096]{2,1,0:T(8,128)(2,1)}, bf16[2,128,1024]{2,1,0:T(8,128)(2,1)}, bf16[48,...) custom-call(bf16[2048,1024]{1,0:T(8,128)(2,1)} %bitcast.3, ...), custom_call_target="tpu_custom_call" | custom-call | tf_op jit(solution)/shard_map/step/pallas_call | solution.py:761
  548.4 1.2 slice.3
  550.3 3.7 fusion.8
  553.9 5.7 %fusion.2 = (bf16[2,32,4096]{2,1,0:T(8,128)(2,1)}, f32[2,32,4096]{2,1,0:T(8,128)}, f32[2,32,4096]{2,1,0:T(8,128)}, bf16[2,32,4096]{2,1,0:T(8,128)(2,1)}, f32[2,32,4096]{2,1,0:T(8,128)}, /*index=5*/f32[2,32,4096]{2,1,0:T(8,128)}) fusion(bf16[2,32,4096]{2,1,0:T(8,128)(2,1)} %refs_2_.1, f32[]{:T(128)} %bitcast.2, bf16[2,32,4096]{2,1,0:T(8,128)(2,1)} %get-tuple-element.13, ...), kind=kLoop, calls=%fused_computation.11 | loop fusion | flops 8912896 | bytes 11534340 | tf_op jit(solution)/shard_map/convert_element_type | solution.py:18

commit v4 on v3

--- a/solution.py
+++ b/solution.py
@@ -8,7 +8,7 @@
 BF, F32 = jnp.bfloat16, jnp.float32
 MESH = pl.DeviceIdType.MESH
 CHUNKS = 48
-SLOTS, OWN, OTHER = 12, 15, 8
+SLOTS, OWN, OTHER, FROMZ = 12, 17, 9, 9
 
 
 def adamw(w, m, v, g):
@@ -45,7 +45,7 @@
 def greet():
     x, y, z, c = place()
     barrier = pltpu.get_barrier_semaphore()
-    others = [(1 - x, y, z, c), (x, 1 - y, z, c), (x, y, z, 1 - c)]
+    others = corners()
     others += [(x, y, (z + hop) % 4, c) for hop in (1, 2, 3)]
     for other in others:
         pl.semaphore_signal(barrier, 1, device_id={"dp": number(*other)}, device_id_type=MESH)
@@ -58,7 +58,7 @@
     )
 
 
-GATHER_AT = (0, 3, 5, 8, 10)
+GATHER_AT = (0, 3, 5, 7, 8)
 DONE = GATHER_AT[-1]
 
 
@@ -117,7 +117,7 @@
                 copy.start()
 
 
-SUM_AT = (0, 1, 3, 6, 8)
+SUM_AT = (0, 1, 4, 7, 9)
 
 
 def wide(ref, *at):
@@ -126,7 +126,7 @@
 
 def sum_stages(k, own, fromtwin, fromfar, fromnear, fromz, sems, out, squares, put):
     f, n, z, c, far, near, ups, twin = route(k)
-    slot, mine = mod(k, SLOTS), mod(k, OWN)
+    slot, mine, zs = mod(k, SLOTS), mod(k, OWN), mod(k, FROMZ)
     every = slice(None)
 
     def pair(i):
@@ -160,7 +160,7 @@
 
     def z_last(hop):
         to = ups[hop][2]
-        return send(fromtwin.at[slot, f, n, to], fromz.at[slot, hop, 0], pair(3), ups[hop])
+        return send(fromtwin.at[slot, f, n, to], fromz.at[zs, hop, 0], pair(3), ups[hop])
 
     def third_near():
         to_far().wait_recv()
@@ -183,11 +183,11 @@
 
     def fifth_near():
         landed(3, out, sems.at[slot, 4])
-        return wide(fromnear, slot, z) + wide(fromz, slot, 0, 0) + wide(fromz, slot, 1, 0) + wide(fromz, slot, 2, 0)
+        return wide(fromnear, slot, z) + wide(fromz, zs, 0, 0) + wide(fromz, zs, 1, 0) + wide(fromz, zs, 2, 0)
 
     def z_first(hop):
         to = ups[hop][2]
-        return send(fromtwin.at[slot, f, every, to], fromz.at[slot, hop], pair(3), ups[hop])
+        return send(fromtwin.at[slot, f, every, to], fromz.at[zs, hop], pair(3), ups[hop])
 
     def near_last():
         return send(fromtwin.at[slot, f, 1 - n, z], fromnear.at[slot, 0], pair(2), near)
@@ -201,7 +201,7 @@
             z_first(hop).start()
 
     def along_z(i):
-        return wide(fromz, slot, 0, i) + wide(fromz, slot, 1, i) + wide(fromz, slot, 2, i)
+        return wide(fromz, zs, 0, i) + wide(fromz, zs, 1, i) + wide(fromz, zs, 2, i)
 
     def fourth_z():
         landed(6, out, sems.at[slot, 4])
@@ -244,22 +244,21 @@
                 pl.when(mod(k, 3) >= 2)(lambda: sum_stages(k, *bufs)[stage][1]())
 
 
+def corners():
+    x, y, z, c = place()
+    return [(x ^ (i // 4), y ^ (i // 2 % 2), z, c ^ (i % 2)) for i in range(1, 8)]
+
+
 def all_squares(squares, total, box, sems):
     x, y, z, c = place()
-    box[0] = jnp.broadcast_to(jnp.sum(squares[...]), (8, 128))
-    for i, other in enumerate([(x, y, z, 1 - c), (1 - x, y, z, c), (x, 1 - y, z, c)]):
-        copy = send(box.at[i], box.at[7 + i], (sems.at[0, i], sems.at[1, i]), other)
-        copy.start()
-        copy.wait()
-        box[i + 1] = box[i] + box[7 + i]
-    copies = [
-        send(box.at[3], box.at[3 + hop], (sems.at[0, 2 + hop], sems.at[1, 2 + hop]), (x, y, (z + hop) % 4, c)) for hop in (1, 2, 3)
-    ]
-    for copy in copies:
-        copy.start()
-    for copy in copies:
-        copy.wait()
-    total[...] = (box[3] + box[5]) + (box[4] + box[6])
+    for at, others in ((0, corners()), (8, [(x, y, (z + hop) & 3, c) for hop in (1, 2, 3)])):
+        box[at] = jnp.broadcast_to(jnp.sum(squares[...]), (8, 128)) if at == 0 else sum(box[i] for i in range(8))
+        for i, other in enumerate(others):
+            send(box.at[at], box.at[at + 1 + i], (sems.at[0, at // 8], sems.at[1, at // 8]), other).start()
+        some = box.at[pl.ds(at + 1, len(others))]
+        for i in range(2):
+            pltpu.make_async_copy(some, some, sems.at[i, at // 8]).wait()
+    total[0, 0] = jnp.max(sum(box[i] for i in range(8, 12)))
 
 
 NN, NT, TN = (((1,), (0,)), ((), ())), (((1,), (1,)), ((), ())), (((0,), (0,)), ((), ()))
@@ -305,11 +304,11 @@
 
 
 def step_kernel(*refs):
-    (x_in, dy_in), shards = refs[0:2], refs[2:5]
+    (x_in, dy_in), shards = [ref.at[0] for ref in refs[0:2]], refs[2:5]
     total, grads, whole = refs[5], refs[6:9], refs[9]
-    acts, silus, slopes, douts, hidden, h1, a0 = refs[10:17]
-    A, B, D, W, F, S, pack, own, fromtwin, fromfar, fromnear, fromz, squares, box = refs[17:31]
-    gsems, glocal, ssems, last, load, tiles = refs[31:37]
+    acts, silus, slopes, douts, h1, a0 = refs[10:16]
+    A, B, D, W, F, S, pack, own, fromtwin, fromfar, fromnear, fromz, squares, box = refs[16:30]
+    gsems, glocal, ssems, last, load, tiles = refs[30:36]
     find()
     x, y, z, c = place()
     copy = pltpu.make_async_copy
@@ -386,16 +385,21 @@
         tick(4 + t)
     copy(A, a0, load.at[0]).wait()
 
-    def wide_quarter(n, i, q, b):
-        def part(at):
-            blk, k = at // 2, 32 * n + 4 * q + 2 * (at % 2) + i
-            bx, by = blk // 2, blk % 2
-            for j in range(4):
-                cut = pl.ds(pl.multiple_of(at % 2 * 512 + 128 * j, 128), 128)
-                src = whole.at[k, bx + i * (by - bx), by + i * (bx - by), :, :, j]
-                copy(src, W.at[b].reshape(4, 4, 2, 32, 1024).at[blk, :, :, :, cut], load.at[2 + b]).start()
-
-        loop(8, part)
+    def wide_half(n, q, h):
+        def part(blk):
+            bx, by = div(blk, 2), mod(blk, 2)
+            for i in range(2):
+                k = 32 * n + 4 * q + 2 * h + i
+                for j in range(4):
+                    cut = pl.ds(512 * h + 128 * j, 128)
+                    src = whole.at[k, bx + i * (by - bx), by + i * (bx - by), :, :, j]
+                    copy(src, W.at[i].reshape(4, 4, 2, 32, 1024).at[blk, :, :, :, cut], load.at[2 + h]).start()
+
+        loop(4, part)
+
+    def half_loaded(h):
+        part = W.at[:, :, pl.ds(512 * h, 512)]
+        copy(part, part, load.at[2 + h]).wait()
 
     def tall_quarter(n, q, b):
         def part(j):
@@ -411,10 +415,6 @@
 
     def phase_gu0():
         def gate_up_0(q):
-            wide_quarter(0, 0, q, 0)
-            wide_quarter(0, 1, q, 1)
-            loaded(0)
-            loaded(1)
             b = q % 2
 
             @pl.when(q >= 2)
@@ -422,8 +422,20 @@
                 copy(D.at[b], acts.at[0, q - 2], load.at[4 + b]).wait()
 
             def tile(i):
-                ticks_at(4 * q + i, DONE + 4, 16)
-                m, n, e = i // 2, i % 2, i % 2
+                for j in range(16):
+                    pl.when(4 * q + i == j)(lambda j=j: tick(DONE + 4 + 5 * (j // 4) + (0, 1, 3, 4)[j % 4]))
+                n, m, e = i // 2, i % 2, i % 2
+
+                @pl.when(i == 0)
+                def _():
+                    wide_half(0, q, 1)
+                    half_loaded(0)
+
+                @pl.when(i == 2)
+                def _():
+                    half_loaded(1)
+                    pl.when(q < 3)(lambda: wide_half(0, q + 1, 0))
+
                 number_of = 4 * q + i
 
                 @pl.when(number_of >= 2)
@@ -432,6 +444,8 @@
                     copy(F.at[2 + e], slopes.at[number_of - 2], tiles.at[1, e]).wait()
 
                 def part(j):
+                    for at in range(4):
+                        pl.when(jnp.logical_and(q == at, 2 * i + j == 3))(lambda at=at: tick(DONE + 6 + 5 * at))
                     here = half(j)
                     there = pl.ds(pl.multiple_of(m * 1024 + j * 512, 512), 512)
                     gate = dot(A[there], W[0, :, half(n)], NN)
@@ -449,6 +463,7 @@
             loop(4, tile)
             copy(D.at[b], acts.at[0, q], load.at[4 + b]).start()
 
+        wide_half(0, 0, 0)
         loop(4, gate_up_0)
         for e in range(2):
             copy(F.at[e], silus.at[14 + e], tiles.at[0, e]).wait()
@@ -456,8 +471,6 @@
             copy(D.at[e], acts.at[0, 2 + e], load.at[4 + e]).wait()
 
     phase_gu0()
-    for t in range(4):
-        tick(DONE + 20 + t)
 
     def act_quarter(n, q, b):
         return copy(acts.at[n, q], D.at[b], load.at[4 + b])
@@ -524,8 +537,8 @@
                 tall_quarter(1, q + 1, 1 - b)
 
             def tile(i):
-                ticks_at(4 * q + i, DONE + 32, 4, 4)
-                m, n, e = i // 2, i % 2, i % 2
+                ticks_at(4 * q + i, DONE + 32, 6, 3)
+                n, m, e = i // 2, i % 2, i % 2
                 number_of = 4 * q + i
 
                 @pl.when(number_of >= 2)
@@ -545,23 +558,24 @@
     copy(D.at[1], h1, load.at[0]).wait()
 
     def wide_gradient(k, i):
-        keep_wide(own, k + i, dot(A[...], D[i // 2, :, half(i % 2)], TN), c)
+        for n in range(2):
+            keep_wide(own, k + 2 * i + n, dot(A[...], D[i, :, pl.ds(512 * n, 512)], TN), c)
 
     def phase_l1():
-        wide_quarter(1, 0, 0, 0)
-        wide_quarter(1, 1, 0, 1)
+        wide_half(1, 0, 0)
+        wide_half(1, 0, 1)
 
         def layer_1(q):
-            loaded(0)
-            loaded(1)
+            half_loaded(0)
             pl.when(q == 1)(lambda: sent_all(1))
             copy(douts.at[4 * q], S.at[0], tiles.at[0, 0]).start()
 
             def tile(i):
                 for j in range(6):
-                    pl.when(4 * q + i == 4 * (j // 2) + 2 * (j % 2) + 1)(lambda j=j: tick(DONE + 36 + 4 * (j // 2) + j % 2))
-                sum_at(i % 2 == 1, 4 * q + i // 2 - 3)
-                m, n, e = i // 2, i % 2, i % 2
+                    pl.when(4 * q + i == 4 * (j // 2) + 2 * (j % 2) + 1)(lambda j=j: tick(DONE + 38 + 4 * (j // 2) + j % 2))
+                sum_at(i % 2 == 0, 4 * q + i // 2 - 3)
+                n, m, e = i // 2, i % 2, i % 2
+                pl.when(i == 2)(lambda: half_loaded(1))
                 number_of = 4 * q + i
                 copy(douts.at[number_of], S.at[e], tiles.at[0, e]).wait()
 
@@ -590,24 +604,27 @@
 
             loop(4, tile)
 
-            for i in range(2):
-                copy(D.at[i], hidden.at[2 * q + i], load.at[4 + i]).start()
+            def back(m):
+                for j in range(3):
+                    pl.when(jnp.logical_and(q == j, m == 1))(lambda j=j: tick(DONE + 40 + 4 * j))
+                sum_at(m == 0, 4 * q - 1)
+                for n in range(2):
+                    cut = pl.ds(512 * n, 512)
+                    part = dot(D[0, rows(m)], W[0, cut], NT) + dot(D[1, rows(m)], W[1, cut], NT)
+                    F[2 * m + n] = jnp.where(q > 0, F[2 * m + n], 0) + part
+
+            loop(2, back)
 
             def part(i):
-                for j in range(6):
-                    pl.when(4 * q + i == 4 * (j // 2) + 2 * (j % 2))(lambda j=j: tick(DONE + 38 + 4 * (j // 2) + j % 2))
-
-                @pl.when(jnp.logical_and(q < 3, i == 3))
-                def _():
-                    wide_quarter(1, 0, q + 1, 0)
-                    wide_quarter(1, 1, q + 1, 1)
-
+                for j in range(2):
+                    pl.when(jnp.logical_and(q == j, i == 1))(lambda j=j: tick(DONE + 41 + 4 * j))
+
+                for h in range(2):
+                    pl.when(jnp.logical_and(q < 3, i == h))(lambda h=h: wide_half(1, q + 1, h))
                 wide_gradient(4 * q, i)
-                sum_at(i % 2 == 1, 4 * q + i // 2 - 1)
-
-            loop(4, part)
-            for i in range(2):
-                copy(D.at[i], hidden.at[2 * q + i], load.at[4 + i]).wait()
+                sum_at(i == 0, 4 * q)
+
+            loop(2, part)
 
         loop(4, layer_1)
         for e in range(2):
@@ -622,50 +639,19 @@
         for j in range(4):
             keep_tall(own, k + 4 * p + j, q, r[:, 128 * j : 128 * j + 128], c)
 
-    def back_part(i):
-        return copy(hidden.at[i], D.at[0], load.at[4])
-
-    def phase_back():
-        def start(i):
-            back_part(i).start()
-
-            @pl.when(i % 2 == 0)
-            def _():
-                wide_quarter(1, 0, i // 2, 0)
-
-            @pl.when(i % 2 == 1)
-            def _():
-                wide_quarter(1, 1, i // 2, 1)
-
-        start(0)
-        act_quarter(1, 0, 1).start()
-
-        def back(i):
-            back_part(i).wait()
-            loaded(i % 2)
-
-            def tile(j):
-                m, n = j // 2, j % 2
-                part = dot(D[0, rows(m)], W[i % 2, half(n)], NT)
-
-                @pl.when(i == 0)
-                def _():
-                    F[j] = part
-
-                @pl.when(i > 0)
-                def _():
-                    F[j] += part
-
-            loop(4, tile)
-            pl.when(i < 7)(lambda: start(i + 1))
-            act_quarter(1, i % 4, 1).wait()
-            tall_part(1, 16, i)
-            pl.when(i < 7)(lambda: act_quarter(1, (i + 1) % 4, 1).start())
-            sum_tick(13 + i, bufs)
-
-        loop(8, back)
-
-    phase_back()
+    def tall_gradient(n, k, t, places):
+        act_quarter(n, 0, 0).start()
+
+        def part(i):
+            b = i % 2
+            act_quarter(n, i % 4, b).wait()
+            pl.when(i < 7)(lambda: act_quarter(n, (i + 1) % 4, 1 - b).start())
+            tall_part(b, k, i)
+            sum_at(sum((i == p).astype(jnp.int32) for p in places) > 0, t + sum((i > p).astype(jnp.int32) for p in places))
+
+        loop(8, part)
+
+    tall_gradient(1, 16, 13, (0, 1, 3, 4, 6, 7))
 
     copy(h1, D.at[0], load.at[0]).start()
     copy(a0, A, load.at[1]).start()
@@ -688,22 +674,10 @@
 
         loop(16, norm_back)
 
-    sum_tick(21, bufs)
+    sum_tick(19, bufs)
     phase_nback()
-    sum_tick(22, bufs)
-    def phase_tall0():
-        act_quarter(0, 0, 0).start()
-
-        def part(i):
-            b = i % 2
-            act_quarter(0, i % 4, b).wait()
-            pl.when(i < 7)(lambda: act_quarter(0, (i + 1) % 4, 1 - b).start())
-            tall_part(b, 24, i)
-            sum_at(i % 2 == 1, 23 + i // 2)
-
-        loop(8, part)
-
-    phase_tall0()
+    sum_tick(20, bufs)
+    tall_gradient(0, 24, 21, (0, 1, 3, 5, 7))
 
     def kept_tile(number_of, e):
         return (
@@ -726,8 +700,8 @@
                 tall_quarter(0, q + 1, 1 - b)
 
             def tile(i):
-                sum_at(i % 2 == 1, 27 + 5 * q + i // 2)
-                m, n, e = i // 2, i % 2, i % 2
+                sum_at(i != 1, 26 + 5 * q + i // 2 + i // 3)
+                n, m, e = i // 2, i % 2, i % 2
                 number_of = 4 * q + i
                 for one in kept_tile(number_of, e):
                     one.wait()
@@ -737,21 +711,24 @@
                     for one in kept_tile(number_of + 1, 1 - e):
                         one.start()
 
-                by_act = dot(B[rows(m)], W[b, half(n)], NT).astype(BF).astype(F32)
-                D[1, rows(m), half(n)] = (by_act * F[e]).astype(BF)
-                D[0, rows(m), half(n)] = (by_act * F[2 + e]).astype(BF)
+                for part in range(2):
+                    here = pl.ds(512 * part, 512)
+                    there = pl.ds(pl.multiple_of(m * 1024 + 512 * part, 512), 512)
+                    by_act = dot(B[there], W[b, half(n)], NT).astype(BF).astype(F32)
+                    D[1, there, half(n)] = (by_act * F[e, here]).astype(BF)
+                    D[0, there, half(n)] = (by_act * F[2 + e, here]).astype(BF)
 
             loop(4, tile)
             def part(i):
-                wide_gradient(32 + 4 * q, i)
-                sum_at(i != 1, 29 + 5 * q + (i + 1) // 2)
+                sum_at(jnp.logical_or(i == 1, i == 2), 28 + 5 * q + i)
+                keep_wide(own, 32 + 4 * q + i, dot(A[...], D[i // 2, :, half(i % 2)], TN), c)
 
             loop(4, part)
 
         loop(4, layer_0)
 
     phase_l0()
-    loop(SUM_AT[-1] + 1, lambda t: sum_tick(CHUNKS - 1 + t, bufs))
+    loop(SUM_AT[-1] + 2, lambda t: sum_tick(CHUNKS - 2 + t, bufs))
     all_squares(squares, total, box, last)
     copy(pack, pack, glocal.at[0]).wait()
 
@@ -761,7 +738,7 @@
     results = pl.pallas_call(
         step_kernel,
         name="step",
-        out_shape=[shape((8, 128), F32)]
+        out_shape=[shape((1, 1), F32)]
         + [shape(w.shape, BF) for w in weights]
         + [
             shape((CHUNKS, 2, 2, 4, 2) + block, BF),
@@ -769,12 +746,11 @@
             shape((16, 1024, 512), F32),
             shape((16, 1024, 512), F32),
             shape((16, 1024, 512), BF),
-            shape((8, 2048, 1024), BF),
             shape((2048, 1024), BF),
             shape((2048, 1024), BF),
         ],
         in_specs=[hbm] * 5,
-        out_specs=[pl.BlockSpec(memory_space=pltpu.VMEM)] + [hbm] * 11,
+        out_specs=[pl.BlockSpec(memory_space=pltpu.SMEM)] + [hbm] * 10,
         scratch_shapes=[
             pltpu.VMEM((2048, 1024), BF),
             pltpu.VMEM((2048, 1024), BF),
@@ -787,13 +763,13 @@
             pltpu.VMEM((SLOTS, 2, 2, 4) + block, BF),
             pltpu.VMEM((SLOTS, 2, 4) + block, BF),
             pltpu.VMEM((SLOTS, 4) + block, BF),
-            pltpu.VMEM((SLOTS, 3, 2) + block, BF),
+            pltpu.VMEM((FROMZ, 3, 2) + block, BF),
             pltpu.VMEM((8, 128), F32),
-            pltpu.VMEM((10, 8, 128), F32),
+            pltpu.VMEM((12, 8, 128), F32),
             pltpu.SemaphoreType.DMA((CHUNKS, 4)),
             pltpu.SemaphoreType.DMA((4,)),
             pltpu.SemaphoreType.DMA((SLOTS, 6)),
-            pltpu.SemaphoreType.DMA((2, 6)),
+            pltpu.SemaphoreType.DMA((2, 2)),
             pltpu.SemaphoreType.DMA((6,)),
             pltpu.SemaphoreType.DMA((2, 2)),
         ],
@@ -805,7 +781,7 @@
 def solution(mesh):
     def step(x, dy, *arrays):
         weights, m, v = (arrays[i : i + 3] for i in (0, 3, 6))
-        squares, mine = stepped(x[0], dy[0], weights)
+        squares, mine = stepped(x, dy, weights)
         count = 32 * sum(g.size for g in mine)
         factor = jnp.minimum(1.0, 0.5 * lax.rsqrt(squares[0, 0] / count + 1e-30))
         new = [adamw(w.astype(F32), m, v, g.astype(F32) * factor) for w, m, v, g in zip(weights, m, v, mine, strict=True)]

time: 561 us -> 525 us (0.936)
  Pallas kernels: 548 us -> 514 us
    pallas_call x1, Pallas kernels: 548 us -> 514 us  [stepped(): pl.pallas_call(step_kernel, name='step', out_shape=[shape((1, 1), F32)] +...]
where the time goes in v4:
time: 525 us
  Pallas kernels  514 us (98%)
  other arithmetic  9.37 us (2%)
    pallas_call x1, Pallas kernels, stepped(): pl.pallas_call(step_kernel, name='step', out_shape=[shape((1, 1), F32)] +...  514 us

profile of v4, /device:TPU:0, one launch (start us, length us, event | category | flops | bytes accessed | tf_op | source)
XLA Modules:
  0.0 524.9 jit_solution(1473518670630192990)
XLA Ops:
  0.6 514.2 %step.1 = (f32[1,1]{1,0:T(1,128)}, bf16[2,32,4096]{2,1,0:T(8,128)(2,1)}, bf16[2,32,4096]{2,1,0:T(8,128)(2,1)}, bf16[2,128,1024]{2,1,0:T(8,128)(2,1)}, bf16[48,2,...) custom-call(bf16[1,2048,1024]{2,1,0:T(8,128)(2,1)} %refs_0_.1, ...), custom_call_target="tpu_custom_call" | custom-call | tf_op jit(solution)/shard_map/step/pallas_call | solution.py:738
  515.5 3.7 fusion.8
  519.2 5.7 %fusion.2 = (bf16[2,32,4096]{2,1,0:T(8,128)(2,1)}, f32[2,32,4096]{2,1,0:T(8,128)}, f32[2,32,4096]{2,1,0:T(8,128)}, bf16[2,32,4096]{2,1,0:T(8,128)(2,1)}, f32[2,32,4096]{2,1,0:T(8,128)}, /*index=5*/f32[2,32,4096]{2,1,0:T(8,128)}) fusion(bf16[2,32,4096]{2,1,0:T(8,128)(2,1)} %refs_2_.1, f32[]{:T(128)} %bitcast, bf16[2,32,4096]{2,1,0:T(8,128)(2,1)} %get-tuple-element.13, ...), kind=kLoop, calls=%fused_computation.11 | loop fusion | flops 8912896 | bytes 11534340 | tf_op jit(solution)/shard_map/convert_element_type | solution.py:18

commit v5 on v4

--- a/solution.py
+++ b/solution.py
@@ -49,7 +49,10 @@
     others += [(x, y, (z + hop) % 4, c) for hop in (1, 2, 3)]
     for other in others:
         pl.semaphore_signal(barrier, 1, device_id={"dp": number(*other)}, device_id_type=MESH)
-    pl.semaphore_wait(barrier, len(others))
+
+
+def greeted():
+    pl.semaphore_wait(pltpu.get_barrier_semaphore(), 10)
 
 
 def send(src, dst, sems, where):
@@ -68,7 +71,7 @@
     f, n = x + color * (y - x), y + color * (x - y)
     far = (x + (1 - color) * (1 - 2 * x), y + color * (1 - 2 * y), z, c)
     near = (x + color * (1 - 2 * x), y + (1 - color) * (1 - 2 * y), z, c)
-    ups = [(x, y, (z + hop) & 3, c) for hop in (1, 2, 3)]
+    ups = [(x, y, (z + hop) & 3, c) for hop in (1, 3, 2)]
     return f, n, z, c, far, near, ups, (x, y, z, 1 - c)
 
 
@@ -315,18 +318,18 @@
 
     def packed(k):
         if 16 <= k < 32:
-            return [copy(shards[2].at[k // 24].reshape(4, 32, 1024).at[:, :, pl.ds(k % 8 * 128, 128)], pack.at[k], glocal.at[0])]
+            return [copy(shards[2].at[k // 24].reshape(4, 32, 1024).at[:, :, pl.ds(k % 8 * 128, 128)], pack.at[k], glocal.at[0 if k > 3 else 4])]
         first = (k % 32) // 4 * 1024 + (k % 4) // 2 * 512
-        return [copy(shards[k % 2].at[k // 32, :, pl.ds(first + 128 * j, 128)], pack.at[k, j], glocal.at[0]) for j in range(4)]
-
+        return [copy(shards[k % 2].at[k // 32, :, pl.ds(first + 128 * j, 128)], pack.at[k, j], glocal.at[0 if k > 3 else 4]) for j in range(4)]
+
+    greet()
     for k in range(CHUNKS):
         for one in packed(k):
             one.start()
     copy(x_in, D.at[0], load.at[0]).start()
     copy(dy_in, B, load.at[1]).start()
     squares[...] = jnp.zeros_like(squares)
-    greet()
-    copy(pack, pack, glocal.at[0]).wait()
+    greeted()
 
     def sent_all(i):
         first = sum(3 if k % 3 < 2 else 1 for k in range(CHUNKS))
@@ -361,13 +364,15 @@
     def sum_at(when, t):
         pl.when(when)(lambda: sum_tick(t, bufs))
 
+    landed(4, pack, glocal.at[4])
     tick(0)
     tick(1)
+    landed(CHUNKS - 4, pack, glocal.at[0])
     for k in range(CHUNKS):
         f, n = route(k)[:2]
         copy(pack.at[k], whole.at[k, f, n, z, c], glocal.at[1]).start()
+    tick(2)
     copy(pack, pack, glocal.at[1]).wait()
-    tick(2)
     tick(3)
     copy(x_in, D.at[0], load.at[0]).wait()
 
@@ -489,6 +494,8 @@
                 tall_quarter(0, q + 1, 1 - b)
                 act_quarter(0, q + 1, 1 - b).start()
 
+            pl.when(q == 3)(lambda: copy(x_in, D.at[0], load.at[0]).start())
+
             def tile(i):
                 ticks_at(4 * q + i, DONE + 24, 8, 2)
                 m, n = i // 2, i % 2
@@ -507,7 +514,7 @@
         loop(4, down_0)
 
     phase_down0()
-    copy(x_in, D.at[0], load.at[0]).start()
+    tall_quarter(1, 0, 0)
     copy(dy_in, B, load.at[1]).wait()
     copy(x_in, D.at[0], load.at[0]).wait()
 
@@ -526,8 +533,6 @@
     copy(D.at[1], h1, load.at[0]).start()
 
     def phase_hid1():
-        tall_quarter(1, 0, 0)
-
         def by_hidden_1(q):
             b = q % 2
             loaded(b)
@@ -621,6 +626,7 @@
 
                 for h in range(2):
                     pl.when(jnp.logical_and(q < 3, i == h))(lambda h=h: wide_half(1, q + 1, h))
+                pl.when(jnp.logical_and(q == 3, i == 1))(lambda: act_quarter(1, 0, 0).start())
                 wide_gradient(4 * q, i)
                 sum_at(i == 0, 4 * q)
 
@@ -639,22 +645,21 @@
         for j in range(4):
             keep_tall(own, k + 4 * p + j, q, r[:, 128 * j : 128 * j + 128], c)
 
-    def tall_gradient(n, k, t, places):
-        act_quarter(n, 0, 0).start()
-
+    def tall_gradient(n, k, t, places, at, then):
         def part(i):
-            b = i % 2
+            b = (i + at) % 2
             act_quarter(n, i % 4, b).wait()
+            pl.when(i == 7)(then)
             pl.when(i < 7)(lambda: act_quarter(n, (i + 1) % 4, 1 - b).start())
             tall_part(b, k, i)
             sum_at(sum((i == p).astype(jnp.int32) for p in places) > 0, t + sum((i > p).astype(jnp.int32) for p in places))
 
         loop(8, part)
 
-    tall_gradient(1, 16, 13, (0, 1, 3, 4, 6, 7))
-
-    copy(h1, D.at[0], load.at[0]).start()
     copy(a0, A, load.at[1]).start()
+    tall_gradient(1, 16, 13, (0, 1, 3, 4, 6, 7), 0, lambda: copy(h1, D.at[0], load.at[0]).start())
+
+    act_quarter(0, 0, 1).start()
     copy(h1, D.at[0], load.at[0]).wait()
 
     def phase_nback():
@@ -677,20 +682,19 @@
     sum_tick(19, bufs)
     phase_nback()
     sum_tick(20, bufs)
-    tall_gradient(0, 24, 21, (0, 1, 3, 5, 7))
-
     def kept_tile(number_of, e):
         return (
             copy(silus.at[number_of], F.at[e], tiles.at[0, e]),
             copy(slopes.at[number_of], F.at[2 + e], tiles.at[1, e]),
         )
 
+    tall_quarter(0, 0, 0)
+    for one in kept_tile(0, 0):
+        one.start()
+    tall_gradient(0, 24, 21, (0, 1, 3, 5, 7), 1, lambda: None)
+
     copy(a0, A, load.at[1]).wait()
     def phase_l0():
-        tall_quarter(0, 0, 0)
-        for one in kept_tile(0, 0):
-            one.start()
-
         def layer_0(q):
             b = q % 2
             loaded(b)
@@ -720,7 +724,7 @@
 
             loop(4, tile)
             def part(i):
-                sum_at(jnp.logical_or(i == 1, i == 2), 28 + 5 * q + i)
+                sum_at(jnp.logical_or(jnp.logical_or(i == 1, i == 2), jnp.logical_and(q == 3, i == 3)), 28 + 5 * q + i)
                 keep_wide(own, 32 + 4 * q + i, dot(A[...], D[i // 2, :, half(i % 2)], TN), c)
 
             loop(4, part)
@@ -728,7 +732,7 @@
         loop(4, layer_0)
 
     phase_l0()
-    loop(SUM_AT[-1] + 2, lambda t: sum_tick(CHUNKS - 2 + t, bufs))
+    loop(SUM_AT[-1] + 1, lambda t: sum_tick(CHUNKS - 1 + t, bufs))
     all_squares(squares, total, box, last)
     copy(pack, pack, glocal.at[0]).wait()
 
@@ -767,7 +771,7 @@
             pltpu.VMEM((8, 128), F32),
             pltpu.VMEM((12, 8, 128), F32),
             pltpu.SemaphoreType.DMA((CHUNKS, 4)),
-            pltpu.SemaphoreType.DMA((4,)),
+            pltpu.SemaphoreType.DMA((5,)),
             pltpu.SemaphoreType.DMA((SLOTS, 6)),
             pltpu.SemaphoreType.DMA((2, 2)),
             pltpu.SemaphoreType.DMA((6,)),

time: 525 us -> 513 us (0.977)
  Pallas kernels: 514 us -> 502 us
    pallas_call x1, Pallas kernels: 514 us -> 502 us  [stepped(): pl.pallas_call(step_kernel, name='step', out_shape=[shape((1, 1), F32)] +...]
where the time goes in v5:
time: 513 us; the launch traced here: 512 us
  Pallas kernels  502 us (98%)
  other arithmetic  9.37 us (2%)
    pallas_call x1, Pallas kernels, stepped(): pl.pallas_call(step_kernel, name='step', out_shape=[shape((1, 1), F32)] +...  502 us

profile of v5, /device:TPU:0, one launch (start us, length us, event | category | flops | bytes accessed | tf_op | source)
XLA Modules:
  0.0 512.4 jit_solution(12335606982820262859)
XLA Ops:
  0.6 501.8 %step.1 = (f32[1,1]{1,0:T(1,128)}, bf16[2,32,4096]{2,1,0:T(8,128)(2,1)}, bf16[2,32,4096]{2,1,0:T(8,128)(2,1)}, bf16[2,128,1024]{2,1,0:T(8,128)(2,1)}, bf16[48,2,...) custom-call(bf16[1,2048,1024]{2,1,0:T(8,128)(2,1)} %refs_0_.1, ...), custom_call_target="tpu_custom_call" | custom-call | tf_op jit(solution)/shard_map/step/pallas_call | solution.py:742
  503.1 3.7 fusion.8
  506.7 5.7 %fusion.2 = (bf16[2,32,4096]{2,1,0:T(8,128)(2,1)}, f32[2,32,4096]{2,1,0:T(8,128)}, f32[2,32,4096]{2,1,0:T(8,128)}, bf16[2,32,4096]{2,1,0:T(8,128)(2,1)}, f32[2,32,4096]{2,1,0:T(8,128)}, /*index=5*/f32[2,32,4096]{2,1,0:T(8,128)}) fusion(bf16[2,32,4096]{2,1,0:T(8,128)(2,1)} %refs_2_.1, f32[]{:T(128)} %bitcast, bf16[2,32,4096]{2,1,0:T(8,128)(2,1)} %get-tuple-element.13, ...), kind=kLoop, calls=%fused_computation.11 | loop fusion | flops 8912896 | bytes 11534340 | tf_op jit(solution)/shard_map/convert_element_type | solution.py:18
